TPU v7x, 32 devices: a whole 2x2x4 slice. The times are simulated.
32 devices in a mesh: replica: 2 (over x), fsdp: 16 (over z, y, core).
Axes of the slice: x: 2, y: 2, z: 4, core: 2. Of those that a mesh axis runs over, the one named last changes fastest.
Arguments:
- tokens: bfloat16 [16384, 1152], P(('replica', 'fsdp')), may hold values from -6 to 6
- cotangent: bfloat16 [16384, 1152], P(('replica', 'fsdp')), may hold values from -6 to 6
- piece_starts: int32 [32, 1], P(('replica', 'fsdp')), may hold values from 0 to 256, as said below
- w_query: bfloat16 [1152, 1024], P('fsdp'), may hold values from -0.1875 to 0.1875
- w_key: bfloat16 [1152, 256], P('fsdp'), may hold values from -0.1875 to 0.1875
- w_value: bfloat16 [1152, 256], P('fsdp'), may hold values from -0.1875 to 0.1875
- w_out: bfloat16 [1024, 1152], P('fsdp'), may hold values from -0.1875 to 0.1875
- w_gate: bfloat16 [1152, 6912], P('fsdp'), may hold values from -0.1875 to 0.1875
- w_up: bfloat16 [1152, 6912], P('fsdp'), may hold values from -0.1875 to 0.1875
- w_down: bfloat16 [6912, 1152], P('fsdp'), may hold values from -0.078125 to 0.078125
- attn_pre_gain: bfloat16 [1152], P('fsdp'), may hold values from 0.5 to 1.5
- query_gain: bfloat16 [256], P('fsdp'), may hold values from 1 to 2.5
- key_gain: bfloat16 [256], P('fsdp'), may hold values from 0.25 to 1.75
- attn_post_gain: bfloat16 [1152], P('fsdp'), may hold values from 0.25 to 1.75
- mlp_pre_gain: bfloat16 [1152], P('fsdp'), may hold values from 0.5 to 1.5
- mlp_post_gain: bfloat16 [1152], P('fsdp'), may hold values from 0.25 to 1.75
Outputs:
- layer_out: bfloat16 [16384, 1152], P(('replica', 'fsdp'))
- input_grad: float32 [16384, 1152], P(('replica', 'fsdp'))
- grad_query: float32 [1152, 1024], P('fsdp')
- grad_key: float32 [1152, 256], P('fsdp')
- grad_value: float32 [1152, 256], P('fsdp')
- grad_out: float32 [1024, 1152], P('fsdp')
- grad_gate: float32 [1152, 6912], P('fsdp')
- grad_up: float32 [1152, 6912], P('fsdp')
- grad_down: float32 [6912, 1152], P('fsdp')
- grad_attn_pre: float32 [1152], P('fsdp')
- grad_query_gain: float32 [256], P('fsdp')
- grad_key_gain: float32 [256], P('fsdp')
- grad_attn_post: float32 [1152], P('fsdp')
- grad_mlp_pre: float32 [1152], P('fsdp')
- grad_mlp_post: float32 [1152], P('fsdp')
Inputs may be any that keep to these rules, and one draw needn't show every extreme that they name: `piece_starts`: each row holds the starts of the 1 image pieces of 256 tokens in one sequence, rising, the pieces disjoint and within the sequence's 512 tokens; the other tokens of the sequence are causal text.
All inputs are finite; a program needn't handle non-finite values.
Results may differ from a plain program's by a relative error of at most 0.018.
Values may be sent and summed in bfloat16 or wider, within the bound.
A program may use at most 320 MiB of HBM per device.

v0:
```python
import jax
import jax.numpy as jnp
from jax import lax
from jax.sharding import PartitionSpec as P

D = 1152
H = 4
HD = 256
FF = 6912
PIECE = 256


epsilon = 1e-06
rope_base = 1000000.0
masked_value = -1e30


def row_scale(values):
    return lax.rsqrt(jnp.mean(values * values, axis=-1, keepdims=True) + epsilon)


def norm_back(values, scale, gain, upstream):
    weighted = upstream * gain
    inner = jnp.mean(weighted * values, axis=-1, keepdims=True)
    grad_values = scale * weighted - values * (scale * scale * scale) * inner
    grad_gain = jnp.sum((upstream * values * scale).reshape(-1, values.shape[-1]), axis=0)
    return (grad_values, grad_gain)


def rope_tables(length, width):
    positions = jnp.arange(length, dtype=jnp.float32)
    freqs = rope_base ** (-jnp.arange(width // 2, dtype=jnp.float32) * 2.0 / width)
    angles = positions[:, None] * freqs[None, :]
    return (jnp.cos(angles), jnp.sin(angles))


def rotate(values, cosine, sine):
    half = values.shape[-1] // 2
    first = values[..., :half]
    second = values[..., half:]
    return jnp.concatenate(
        [first * cosine - second * sine, second * cosine + first * sine], axis=-1
    )


def rotate_back(upstream, cosine, sine):
    half = upstream.shape[-1] // 2
    first = upstream[..., :half]
    second = upstream[..., half:]
    return jnp.concatenate(
        [first * cosine + second * sine, second * cosine - first * sine], axis=-1
    )


def score_mask(rows, columns, starts):
    inside_rows = (rows[None, :] >= starts[:, None]) & (rows[None, :] < starts[:, None] + PIECE)
    inside_cols = (columns[None, :] >= starts[:, None]) & (
        columns[None, :] < starts[:, None] + PIECE
    )
    same = jnp.any(inside_rows[:, :, None] & inside_cols[:, None, :], axis=0)
    return (columns[None, :] <= rows[:, None]) | same


def matmul(left, right):
    return jnp.dot(left, right, preferred_element_type=jnp.float32)


def matmul_back(left, right):
    return lax.dot_general(
        left, right, (((1,), (1,)), ((), ())), preferred_element_type=jnp.float32
    )


def term_maker(left, rights):

    def term(start, count):
        parts = [
            lax.dot_general(
                left, right, (((0,), (0,)), ((), ())), preferred_element_type=jnp.float32
            )
            for right in rights
        ]
        return jnp.concatenate(parts, axis=1)

    return term


def on_device(
    tokens,
    cotangent,
    piece_starts,
    w_query,
    w_key,
    w_value,
    w_out,
    w_gate,
    w_up,
    w_down,
    attn_pre_gain,
    query_gain,
    key_gain,
    attn_post_gain,
    mlp_pre_gain,
    mlp_post_gain,
):
    length = tokens.shape[0]
    starts = piece_starts[0]
    fsdp_count = lax.axis_size("fsdp")
    attn_full = (
        lax.all_gather(w_query, "fsdp", axis=0, tiled=True),
        lax.all_gather(w_key, "fsdp", axis=0, tiled=True),
        lax.all_gather(w_value, "fsdp", axis=0, tiled=True),
        lax.all_gather(w_out, "fsdp", axis=0, tiled=True),
        lax.all_gather(attn_pre_gain, "fsdp", axis=0, tiled=True),
        lax.all_gather(query_gain, "fsdp", axis=0, tiled=True),
        lax.all_gather(key_gain, "fsdp", axis=0, tiled=True),
        lax.all_gather(attn_post_gain, "fsdp", axis=0, tiled=True),
    )
    gain_attn_pre = attn_full[4].astype(jnp.float32)
    gain_query = attn_full[5].astype(jnp.float32)
    gain_key = attn_full[6].astype(jnp.float32)
    gain_attn_post = attn_full[7].astype(jnp.float32)
    inputs = tokens.astype(jnp.float32)
    scale_attn = row_scale(inputs)
    normed_attn = (inputs * scale_attn * gain_attn_pre).astype(jnp.bfloat16)
    query_proj = matmul(normed_attn, attn_full[0]).reshape(length, H, HD)
    key_proj = matmul(normed_attn, attn_full[1])
    value_proj = matmul(normed_attn, attn_full[2])
    cosine, sine = rope_tables(length, HD)
    attn_factor = HD ** (-0.5)
    scale_query = row_scale(query_proj)
    query_low = (
        rotate(query_proj * scale_query * gain_query, cosine[:, None, :], sine[:, None, :])
        * attn_factor
    ).astype(jnp.bfloat16)
    scale_key = row_scale(key_proj)
    key_low = rotate(key_proj * scale_key * gain_key, cosine, sine).astype(jnp.bfloat16)
    value_low = value_proj.astype(jnp.bfloat16)
    count = length // length
    columns = jnp.arange(length, dtype=jnp.int32)
    block_ids = jnp.arange(count, dtype=jnp.int32)
    query_blocks = query_low.reshape(count, length, H, HD)

    def attend(item):
        index, queries = item
        rows = index * length + jnp.arange(length, dtype=jnp.int32)
        allowed = score_mask(rows, columns, starts)
        scores = jnp.einsum("thd,sd->hts", queries, key_low, preferred_element_type=jnp.float32)
        scores = jnp.where(allowed[None], scores, masked_value)
        peak = jnp.max(scores, axis=-1, keepdims=True)
        expo = jnp.exp(scores - peak)
        total = jnp.sum(expo, axis=-1, keepdims=True)
        probs_low = (expo / total).astype(jnp.bfloat16)
        mixed_part = jnp.einsum(
            "hts,sd->thd", probs_low, value_low, preferred_element_type=jnp.float32
        )
        return (mixed_part, (peak + jnp.log(total))[..., 0])

    mixed_parts, logsums = lax.map(attend, (block_ids, query_blocks))
    mixed_low = mixed_parts.reshape(length, H * HD).astype(jnp.bfloat16)
    attn_out = matmul(mixed_low, attn_full[3])
    scale_post = row_scale(attn_out)
    resid = inputs + attn_out * scale_post * gain_attn_post
    mlp_full = (
        lax.all_gather(w_gate, "fsdp", axis=0, tiled=True),
        lax.all_gather(w_up, "fsdp", axis=0, tiled=True),
        lax.all_gather(w_down, "fsdp", axis=0, tiled=True),
        lax.all_gather(mlp_pre_gain, "fsdp", axis=0, tiled=True),
        lax.all_gather(mlp_post_gain, "fsdp", axis=0, tiled=True),
    )
    gain_mlp_pre = mlp_full[3].astype(jnp.float32)
    gain_mlp_post = mlp_full[4].astype(jnp.float32)
    scale_mlp = row_scale(resid)
    normed_mlp = (resid * scale_mlp * gain_mlp_pre).astype(jnp.bfloat16)
    gate = matmul(normed_mlp, mlp_full[0])
    upper = matmul(normed_mlp, mlp_full[1])
    activated, gelu_pull = jax.vjp(lambda values: jax.nn.gelu(values, approximate=True), gate)
    hidden_low = (activated * upper).astype(jnp.bfloat16)
    mlp_out = matmul(hidden_low, mlp_full[2])
    scale_out = row_scale(mlp_out)
    layer_out = (resid + mlp_out * scale_out * gain_mlp_post).astype(jnp.bfloat16)
    upstream = cotangent.astype(jnp.float32)
    grad_mlp_out, grad_mlp_post = norm_back(mlp_out, scale_out, gain_mlp_post, upstream)
    grad_mlp_low = grad_mlp_out.astype(jnp.bfloat16)
    grad_hidden = matmul_back(grad_mlp_low, mlp_full[2])
    grad_gate_low = gelu_pull(grad_hidden * upper)[0].astype(jnp.bfloat16)
    grad_up_low = (grad_hidden * activated).astype(jnp.bfloat16)
    grad_normed_mlp = matmul_back(grad_gate_low, mlp_full[0]) + matmul_back(
        grad_up_low, mlp_full[1]
    )
    grad_resid_part, grad_mlp_pre = norm_back(resid, scale_mlp, gain_mlp_pre, grad_normed_mlp)
    grad_resid = upstream + grad_resid_part
    mlp_in_term = term_maker(normed_mlp, (grad_gate_low, grad_up_low))
    down_term = term_maker(hidden_low, (grad_mlp_low,))
    mlp_in_share = lax.psum_scatter(
        mlp_in_term(jnp.int32(0), lax.axis_size("fsdp") * (D // fsdp_count)),
        "fsdp",
        scatter_dimension=0,
        tiled=True,
    )
    down_share = lax.psum_scatter(
        down_term(jnp.int32(0), lax.axis_size("fsdp") * (FF // fsdp_count)),
        "fsdp",
        scatter_dimension=0,
        tiled=True,
    )
    grad_attn_out, grad_attn_post = norm_back(attn_out, scale_post, gain_attn_post, grad_resid)
    grad_attn_low = grad_attn_out.astype(jnp.bfloat16)
    grad_mixed_low = matmul_back(grad_attn_low, attn_full[3]).astype(jnp.bfloat16)
    grad_blocks = grad_mixed_low.reshape(count, length, H, HD)

    def attend_back(carry, item):
        key_total, value_total = carry
        index, queries, grads, logsum = item
        rows = index * length + jnp.arange(length, dtype=jnp.int32)
        allowed = score_mask(rows, columns, starts)
        scores = jnp.einsum("thd,sd->hts", queries, key_low, preferred_element_type=jnp.float32)
        scores = jnp.where(allowed[None], scores, masked_value)
        probs = jnp.exp(scores - logsum[..., None])
        probs_low = probs.astype(jnp.bfloat16)
        grad_probs = jnp.einsum("thd,sd->hts", grads, value_low, preferred_element_type=jnp.float32)
        value_total = value_total + jnp.einsum(
            "hts,thd->sd", probs_low, grads, preferred_element_type=jnp.float32
        )
        inner = jnp.sum(probs * grad_probs, axis=-1, keepdims=True)
        grad_scores = (probs * (grad_probs - inner)).astype(jnp.bfloat16)
        grad_queries = jnp.einsum(
            "hts,sd->thd", grad_scores, key_low, preferred_element_type=jnp.float32
        )
        key_total = key_total + jnp.einsum(
            "hts,thd->sd", grad_scores, queries, preferred_element_type=jnp.float32
        )
        return ((key_total, value_total), grad_queries)

    zero_rows = jnp.zeros((length, HD), jnp.float32)
    (grad_key_rot, grad_value_act), grad_query_parts = lax.scan(
        attend_back, (zero_rows, zero_rows), (block_ids, query_blocks, grad_blocks, logsums)
    )
    grad_query_act = grad_query_parts.reshape(length, H, HD)
    grad_query_normed = rotate_back(
        grad_query_act * attn_factor, cosine[:, None, :], sine[:, None, :]
    )
    grad_query_proj, grad_query_gain = norm_back(
        query_proj, scale_query, gain_query, grad_query_normed
    )
    grad_key_normed = rotate_back(grad_key_rot, cosine, sine)
    grad_key_proj, grad_key_gain = norm_back(key_proj, scale_key, gain_key, grad_key_normed)
    grad_query_low = grad_query_proj.reshape(length, H * HD).astype(jnp.bfloat16)
    grad_key_low = grad_key_proj.astype(jnp.bfloat16)
    grad_value_low = grad_value_act.astype(jnp.bfloat16)
    grad_normed_attn = (
        matmul_back(grad_query_low, attn_full[0])
        + matmul_back(grad_key_low, attn_full[1])
        + matmul_back(grad_value_low, attn_full[2])
    )
    grad_input_part, grad_attn_pre = norm_back(inputs, scale_attn, gain_attn_pre, grad_normed_attn)
    input_grad = grad_resid + grad_input_part
    attn_in_term = term_maker(normed_attn, (grad_query_low, grad_key_low, grad_value_low))
    out_term = term_maker(mixed_low, (grad_attn_low,))
    attn_in_share = lax.psum_scatter(
        attn_in_term(jnp.int32(0), lax.axis_size("fsdp") * (D // fsdp_count)),
        "fsdp",
        scatter_dimension=0,
        tiled=True,
    )
    out_share = lax.psum_scatter(
        out_term(jnp.int32(0), lax.axis_size("fsdp") * (H * HD // fsdp_count)),
        "fsdp",
        scatter_dimension=0,
        tiled=True,
    )
    gains_all = lax.psum(
        (
            grad_attn_pre,
            grad_query_gain,
            grad_key_gain,
            grad_attn_post,
            grad_mlp_pre,
            grad_mlp_post,
        ),
        ("replica", "fsdp"),
    )
    owner = lax.axis_index("fsdp")
    d_rows = D // fsdp_count
    h_rows = HD // fsdp_count
    gain_shares = (
        lax.dynamic_slice_in_dim(gains_all[0], owner * d_rows, d_rows, 0),
        lax.dynamic_slice_in_dim(gains_all[1], owner * h_rows, h_rows, 0),
        lax.dynamic_slice_in_dim(gains_all[2], owner * h_rows, h_rows, 0),
        lax.dynamic_slice_in_dim(gains_all[3], owner * d_rows, d_rows, 0),
        lax.dynamic_slice_in_dim(gains_all[4], owner * d_rows, d_rows, 0),
        lax.dynamic_slice_in_dim(gains_all[5], owner * d_rows, d_rows, 0),
    )
    results = (
        lax.psum(attn_in_share.astype(jnp.bfloat16), "replica").astype(jnp.float32),
        lax.psum(out_share.astype(jnp.bfloat16), "replica").astype(jnp.float32),
        lax.psum(mlp_in_share.astype(jnp.bfloat16), "replica").astype(jnp.float32),
        lax.psum(down_share.astype(jnp.bfloat16), "replica").astype(jnp.float32),
    )
    attn_in_full = results[0]
    mlp_in_full = results[2]
    qwidth = H * HD
    grad_query = attn_in_full[:, :qwidth]
    grad_key = attn_in_full[:, qwidth : qwidth + HD]
    grad_value = attn_in_full[:, qwidth + HD :]
    grad_gate = mlp_in_full[:, :FF]
    grad_up = mlp_in_full[:, FF:]
    return (
        layer_out,
        input_grad,
        grad_query,
        grad_key,
        grad_value,
        results[1],
        grad_gate,
        grad_up,
        results[3],
        gain_shares[0],
        gain_shares[1],
        gain_shares[2],
        gain_shares[3],
        gain_shares[4],
        gain_shares[5],
    )


def solution(mesh):
    placed = (
        P(("replica", "fsdp"), None),
        P(("replica", "fsdp"), None),
        P(("replica", "fsdp"), None),
        P("fsdp", None),
        P("fsdp", None),
        P("fsdp", None),
        P("fsdp", None),
        P("fsdp", None),
        P("fsdp", None),
        P("fsdp", None),
        P("fsdp"),
        P("fsdp"),
        P("fsdp"),
        P("fsdp"),
        P("fsdp"),
        P("fsdp"),
    )
    return jax.shard_map(
        on_device,
        mesh=mesh,
        in_specs=placed,
        out_specs=(
            P(("replica", "fsdp"), None),
            P(("replica", "fsdp"), None),
            P("fsdp", None),
            P("fsdp", None),
            P("fsdp", None),
            P("fsdp", None),
            P("fsdp", None),
            P("fsdp", None),
            P("fsdp", None),
            P("fsdp"),
            P("fsdp"),
            P("fsdp"),
            P("fsdp"),
            P("fsdp"),
            P("fsdp"),
        ),
        check_vma=False,
    )
```

profile of v0, /device:TPU:0, one launch (start us, length us, event | category | flops | bytes accessed | tf_op | source)
XLA Modules:
  0.0 1775.4 jit_solution(9544685377612976665)
XLA Ops:
  14.8 63.6 %all-reduce.8 = (bf16[1152]{0:T(1024)(128)(2,1)S(1)}, bf16[256]{0:T(256)(128)(2,1)S(1)}, bf16[256]{0:T(256)(128)(2,1)S(1)}, bf16[1152]{0:T(1024)(128)(2,1)S(1)},...) all-reduce(bf16[1152]{0:T(1024)(128)(2,1)S(1)} %dynamic-update-slic, ...), channel_id=1, replica_groups=mesh['replica'=2,'fsdp'=16] {'fsdp'}, use_global_device_ids=true, to_apply=%add | all-reduce | flops 5120 | bytes 20480
  81.0 21.2 %all_gather.41 = bf16[1152,256]{1,0:T(8,128)(2,1)S(1)} all-gather(bf16[72,256]{1,0:T(8,128)(2,1)S(1)} %copy-done.69), channel_id=1, replica_groups=mesh['replica'=2,'fsdp'=16] {'fsdp'}, dimensions={0}, use_global_device_ids=true | all-gather | bytes 626688 | tf_op jit(solution)/shard_map/all_gather | solution.py:111
  104.2 1.8 fusion.56
  108.0 21.2 %all_gather.40 = bf16[1152,256]{1,0:T(8,128)(2,1)S(1)} all-gather(bf16[72,256]{1,0:T(8,128)(2,1)S(1)} %copy-done.70), channel_id=1, replica_groups=mesh['replica'=2,'fsdp'=16] {'fsdp'}, dimensions={0}, use_global_device_ids=true | all-gather | bytes 626688 | tf_op jit(solution)/shard_map/all_gather | solution.py:112
  129.2 1.3 fusion.48
  130.5 3.2 fusion.79
  133.7 2.2 reshape.320
  135.9 2.9 multiply_reduce_fusion.7
  146.2 1.4 fusion.41
  147.6 3.7 multiply_reduce_fusion.6
  153.6 72.0 %all-gather.10.cloned.1.call-done = bf16[1152,6912]{1,0:T(8,128)(2,1)} async-done(((bf16[72,6912]{1,0:T(8,128)(2,1)}), bf16[1152,6912]{1,0:T(8,128)(2,1)}) %all-gather.10.cloned.1.call-update) | async-done | bytes 15925264 | tf_op jit(solution)/shard_map/all_gather | solution.py:165
  225.6 16.0 fusion.86
  241.5 105.8 %all-gather.12.cloned.1.call-done = bf16[1152,6912]{1,0:T(8,128)(2,1)} async-done(((bf16[72,6912]{1,0:T(8,128)(2,1)}), bf16[1152,6912]{1,0:T(8,128)(2,1)}) %all-gather.12.cloned.1.call-update) | async-done | bytes 15925264 | tf_op jit(solution)/shard_map/all_gather | solution.py:166
  347.3 21.5 %multiply_convert_fusion.1 = (bf16[512,6912]{1,0:T(8,128)(2,1)}, f32[512,6912]{1,0:T(8,128)}) fusion(f32[512,6912]{1,0:T(8,128)} %fusion.86, bf16[512,1152]{1,0:T(8,128)(2,1)S(1)} %multiply_convert_fusion.2, bf16[1152,6912]{1,0:T(8,128)(2,1)} %all-gather.12.cloned.1.call-done), kind=kOutput, calls=%fused_computation.11 | convolution fusion | flops 8189116416 | bytes 52494336 | tf_op jit(solution)/shard_map/dot_general | solution.py:65
  368.9 100.2 %all-gather.14.cloned.1.call-done = bf16[6912,1152]{1,0:T(8,128)(2,1)} async-done(((bf16[432,1152]{1,0:T(8,128)(2,1)}), bf16[6912,1152]{1,0:T(8,128)(2,1)}) %all-gather.14.cloned.1.call-update) | async-done | bytes 15925264 | tf_op jit(solution)/shard_map/all_gather | solution.py:167
  469.1 14.5 multiply_reduce_fusion.4
  484.2 2.6 fusion.19
  487.3 28.6 %multiply_convert_fusion = (bf16[512,6912]{1,0:T(8,128)(2,1)}, bf16[512,6912]{1,0:T(8,128)(2,1)}) fusion(f32[512,6912]{1,0:T(8,128)} %fusion.86, f32[512,6912]{1,0:T(8,128)} %get-tuple-element.216, bf16[6912,1152]{1,0:T(8,128)(2,1)} %all-gather.14.cloned.1.call-done, bf16[512,1152]{1,0:T(8,128)(2,1)S(1)} %copy-done.26, f32[512,1152]{1,0:T(8,128)} %copy-done.33, ...), kind=kOutput, calls=%fused_computation.10 | convolution fusion | flops 8242790400 | bytes 61942272 | tf_op jit(solution)/shard_map/dot_general | solution.py:69
  516.0 15.7 fusion.87
  531.8 16.2 multiply_reduce_fusion
  548.0 2.3 multiply_reduce_fusion.1
  552.3 3.7 fusion.89
  558.2 1.8 copy.159
  560.7 1.8 copy.161
  563.3 1.6 convolution_convert_fusion
  566.0 1.5 fusion.7
  567.5 1.3 fusion.9
  570.6 2.2 copy-done.1
  573.3 1.6 copy.158
  578.6 1.4 multiply_add_fusion.2
  585.4 1.4 subtract_convert_fusion.1
  587.8 3.9 fusion.77
  591.7 5.7 pad_maximum_fusion.1
  597.4 8.1 copy.151
  606.3 18.6 %fusion.69 = f32[6912,1152]{1,0:T(8,128)} fusion(bf16[512,6912]{1,0:T(8,128)(2,1)} %get-tuple-element.215, bf16[512,1152]{1,0:T(8,128)(2,1)} %param.17, f32[512,1152]{1,0:T(8,128)} %copy-done.33, f32[512]{0:T(512)S(1)} %copy-done.101, f32[512]{0:T(512)S(1)} %copy-done.100, f32[1152]{0:T(1024)S(1)} %copy-done.81, f32[512]{0:T(512)S(1)} %copy-done.95), kind=kOutput, calls=%fused_computation.148 | convolution fusion | flops 8157855744 | bytes 42478080 | tf_op jit(solution)/shard_map/dot_general | solution.py:78
  625.0 19.7 %fusion.91 = f32[1152,6912]{1,0:T(8,128)} fusion(bf16[512,1152]{1,0:T(8,128)(2,1)} %copy-done.11, bf16[512,6912]{1,0:T(8,128)(2,1)} %get-tuple-element.176), kind=kOutput, calls=%fused_computation.162 | convolution fusion | flops 8153726976 | bytes 40108032 | tf_op jit(solution)/shard_map/dot_general | solution.py:78
  644.7 17.8 %fusion.90 = f32[1152,6912]{1,0:T(8,128)} fusion(bf16[512,1152]{1,0:T(8,128)(2,1)S(1)} %copy-done.12, bf16[512,6912]{1,0:T(8,128)(2,1)} %get-tuple-element.177), kind=kOutput, calls=%fused_computation.161 | convolution fusion | flops 8153726976 | bytes 40108032 | tf_op jit(solution)/shard_map/dot_general | solution.py:78
  662.4 43.9 %pad_maximum_fusion = f32[1152,13824]{1,0:T(8,128)} fusion(f32[1152,6912]{1,0:T(8,128)} %fusion.91, f32[1152,6912]{1,0:T(8,128)} %fusion.90), kind=kLoop, calls=%fused_computation | loop fusion | flops 15925248 | bytes 127401984 | tf_op jit(solution)/shard_map/concatenate | solution.py:83
  706.4 1.6 convert_element_type.142
  708.0 15.5 reduce-scatter.13.cloned.1.call-done
  723.5 1.9 copy.152
  725.5 321.8 %reduce-scatter.11.cloned.1.call-done = f32[432,1152]{1,0:T(8,128)} async-done(((f32[6912,1152]{1,0:T(8,128)}), f32[432,1152]{1,0:T(8,128)}) %reduce-scatter.11.cloned.1.call-update) | async-done | bytes 1990672 | tf_op jit(solution)/shard_map/reduce_scatter | solution.py:201
  1047.3 2.6 convert_element_type.146
  1049.9 607.9 %reduce-scatter.15.cloned.1.call-done = f32[72,13824]{1,0:T(8,128)} async-done(((f32[1152,13824]{1,0:T(8,128)}), f32[72,13824]{1,0:T(8,128)}) %reduce-scatter.15.cloned.1.call-update) | async-done | bytes 3981328
  1657.8 3.6 convert_element_type.144
  1661.4 1.8 reshape.321
  1663.4 2.1 copy.136
  1668.7 1.6 fusion.88
  1671.4 2.9 fusion.28
  1674.3 41.2 %all-reduce.7 = (f32[1152]{0:T(1024)}, f32[256]{0:T(256)}, f32[256]{0:T(256)}, f32[1152]{0:T(1024)}, f32[1152]{0:T(1024)}, /*index=5*/f32[1152]{0:T(1024)}) all-reduce(f32[1152]{0:T(1024)} %get-tuple-element.153, f32[256]{0:T(256)} %fusion.35, f32[256]{0:T(256)} %get-tuple-element.155, ...), channel_id=1, replica_groups=mesh['replica'=2,'fsdp'=16] {'replica','fsdp'}, use_global_device_ids=true, to_apply=%region_24.25 | all-reduce | flops 5120 | bytes 40960 | tf_op jit(solution)/shard_map/psum | solution.py:272
  1715.6 1.2 dynamic_slice.34
  1716.8 1.2 dynamic_slice.35
  1718.1 1.3 dynamic_slice.33
  1719.3 1.3 dynamic_slice.36
  1720.6 1.3 dynamic_slice.37
  1721.9 1.3 dynamic_slice.38
  1723.9 3.7 fusion.25
  1727.5 28.6 %all-reduce.12.cloned.1.call-done = (bf16[72,1536]{0,1:T(8,128)(2,1)}, bf16[72,13824]{1,0:T(8,128)(2,1)}, bf16[64,1152]{1,0:T(8,128)(2,1)}, bf16[432,1152]{1,0:T(8,128)(2,1)}) async-done(((bf16[72,1536]{0,1:T(8,128)(2,1)}, bf16[72,13824]{1,0:T(8,128)(2,1)}, bf16[64,1152]{1,0:T(8,128)(2,1)}, bf16[432,1152]{1,0:T(8,128)(2,1)}), (bf16[72,1536]{0,1:T(8,128)(2,1)}, bf16[72,13824]{1,0:T(8,128)(2,1)}, ...) | async-done | bytes 3354640 | tf_op jit(solution)/shard_map/psum | solution.py:295
  1756.1 1.7 fusion.85
  1758.8 1.8 copy.141
  1760.6 1.6 copy.140
  1763.1 1.6 convert_element_type.143
  1764.7 1.4 convert_element_type.147
  1766.2 2.2 fusion.84
  (314 shorter events, 49.5 us)
Async XLA Ops:
  7.2 4.2 copy-start.109
  7.2 6.1 copy-start.103
  7.2 6.3 copy-start.104
  7.2 6.6 copy-start.105
  7.2 6.8 copy-start.106
  7.2 7.0 copy-start.107
  7.2 7.3 copy-start.108
  7.3 72.9 %copy-start.9 = (bf16[512,1152]{1,0:T(8,128)(2,1)S(1)}, bf16[512,1152]{1,0:T(8,128)(2,1)}, u32[]{:S(2)}) copy-start(bf16[512,1152]{1,0:T(8,128)(2,1)} %param.16) | copy-start | bytes 3538948
  7.3 73.8 %copy-start.69 = (bf16[72,256]{1,0:T(8,128)(2,1)S(1)}, bf16[72,256]{1,0:T(8,128)(2,1)}, u32[]{:S(2)}) copy-start(bf16[72,256]{1,0:T(8,128)(2,1)} %param.20) | copy-start | bytes 110596
  7.3 123.2 %all-gather.6.cloned.1.call-start = ((), (), s32[]{:S(2)}) async-start(), calls=%async_computation.4 | async-start | bytes 2506752 | tf_op jit(solution)/shard_map/all_gather | solution.py:110
  8.0 139.6 %all-gather.8.cloned.1.call-start = ((), (), s32[]{:S(2)}) async-start(), calls=%async_computation.5 | async-start | bytes 2506752 | tf_op jit(solution)/shard_map/all_gather | solution.py:113
  8.8 216.8 %all-gather.10.cloned.1.call-start = ((), (), s32[]{:S(2)}) async-start(), calls=%async_computation.6 | async-start | bytes 16920576 | tf_op jit(solution)/shard_map/all_gather | solution.py:165
  9.5 337.8 %all-gather.12.cloned.1.call-start = ((), (), s32[]{:S(2)}) async-start(), calls=%async_computation.7 | async-start | bytes 16920576 | tf_op jit(solution)/shard_map/all_gather | solution.py:166
  10.1 459.0 %all-gather.14.cloned.1.call-start = ((), (), s32[]{:S(2)}) async-start(), calls=%async_computation.8 | async-start | bytes 16920576 | tf_op jit(solution)/shard_map/all_gather | solution.py:167
  10.7 695.7 %reduce-scatter.9.cloned.1.call-start = ((), (), s32[]{:S(2)}) async-start(), calls=%async_computation.9 | async-start | bytes 5013504 | tf_op jit(solution)/shard_map/reduce_scatter | solution.py:266
  78.3 25.2 %copy-start.89 = (f32[256]{0:T(256)}, f32[256]{0:T(256)S(1)}, u32[]{:S(2)}) copy-start(f32[256]{0:T(256)S(1)} %convert_element_type.116) | copy-start | bytes 3076
  78.9 51.5 %copy-start.64 = (f32[1152]{0:T(1024)}, f32[1152]{0:T(1024)S(1)}, u32[]{:S(2)}) copy-start(f32[1152]{0:T(1024)S(1)} %convert_element_type.113) | copy-start | bytes 13828
  78.9 73.1 %copy-start.62 = (f32[1152]{0:T(1024)}, f32[1152]{0:T(1024)S(1)}, u32[]{:S(2)}) copy-start(f32[1152]{0:T(1024)S(1)} %convert_element_type.123) | copy-start | bytes 13828
  80.1 24.1 %copy-start.98 = (f32[128]{0:T(128)}, f32[128]{0:T(128)S(1)}, u32[]{:S(2)}) copy-start(f32[128]{0:T(128)S(1)} %multiply_power_fusion) | copy-start | bytes 1540
  81.0 48.2 %copy-start.83 = (f32[512]{0:T(512)}, f32[512]{0:T(512)S(1)}, u32[]{:S(2)}) copy-start(f32[512]{0:T(512)S(1)} %get-tuple-element.196) | copy-start | bytes 6148
  102.2 3.9 copy-start.41
  102.9 5.1 copy-start.70
  108.0 36.9 %copy-start.29 = (pred[512,512]{0,1:T(8,128)(4,1)}, pred[512,512]{0,1:T(8,128)(4,1)S(1)}, u32[]{:S(2)}) copy-start(pred[512,512]{0,1:T(8,128)(4,1)S(1)} %fusion.52) | copy-start | bytes 786436
  133.7 6.8 copy-start
  147.6 3.7 copy-start.24
  153.3 88.2 %copy-start.86 = (f32[512]{0:T(512)}, f32[512]{0:T(512)S(1)}, u32[]{:S(2)}) copy-start(f32[512]{0:T(512)S(1)} %get-tuple-element.202) | copy-start | bytes 6148
  153.6 193.8 %copy-start.11 = (bf16[512,1152]{1,0:T(8,128)(2,1)}, bf16[512,1152]{1,0:T(8,128)(2,1)S(1)}, u32[]{:S(2)}) copy-start(bf16[512,1152]{1,0:T(8,128)(2,1)S(1)} %multiply_convert_fusion.2) | copy-start | bytes 3538948
  469.1 15.1 copy-start.26
  469.1 15.1 copy-start.80
  483.6 3.2 copy-start.33
  484.2 2.6 copy-start.94
  516.0 15.7 copy-start.23
  516.0 15.7 copy-start.87
  531.7 16.3 copy-start.6
  531.7 16.3 copy-start.63
  531.7 16.3 copy-start.72
  531.7 16.3 copy-start.97
  556.0 167.5 %reduce-scatter.13.cloned.1.call-start = ((), (), s32[]{:S(2)}) async-start(), calls=%async_computation.11 | async-start | bytes 7520256
  557.4 2.6 copy-start.38
  560.6 2.6 copy-start.40
  563.3 2.4 copy-start.3
  563.3 2.5 copy-start.30
  563.3 2.8 copy-start.61
  564.8 2.7 copy-start.43
  570.3 2.5 copy-start.1
  570.3 2.5 copy-start.92
  570.5 2.7 copy-start.13
  570.6 2.7 copy-start.15
  577.8 3.0 copy-start.93
  577.8 3.1 copy-start.4
  578.6 2.4 copy-start.44
  581.0 2.7 copy-start.19
  582.4 3.0 copy-start.18
  582.4 3.0 copy-start.88
  605.6 441.7 %reduce-scatter.11.cloned.1.call-start = ((), (), s32[]{:S(2)}) async-start(), calls=%async_computation.10 | async-start | bytes 33841152 | tf_op jit(solution)/shard_map/reduce_scatter | solution.py:201
  624.9 1032.9 %reduce-scatter.15.cloned.1.call-start = ((), (), s32[]{:S(2)}) async-start(), calls=%async_computation.12 | async-start | bytes 67682304
  625.0 19.7 %copy-start.12 = (bf16[512,1152]{1,0:T(8,128)(2,1)S(1)}, bf16[512,1152]{1,0:T(8,128)(2,1)}, u32[]{:S(2)}) copy-start(bf16[512,1152]{1,0:T(8,128)(2,1)} %copy-done.11) | copy-start | bytes 3538948
  706.3 1049.8 %all-reduce.12.cloned.1.call-start = ((), (), s32[]{:S(2)}) async-start(), calls=%async_computation.13 | async-start | bytes 7053312 | tf_op jit(solution)/shard_map/psum | solution.py:295
  1663.4 2.8 copy-start.16
  1666.2 2.6 copy-start.102
  1671.4 2.9 copy-start.75
  1671.4 52.4 %copy-start.8 = (f32[512,1152]{1,0:T(8,128)S(1)}, f32[512,1152]{1,0:T(8,128)}, u32[]{:S(2)}) copy-start(f32[512,1152]{1,0:T(8,128)} %copy-done.7) | copy-start | bytes 7077892
  1756.1 8.6 copy-start.53
  1758.8 7.4 copy-start.22
  (56 other events, 81.6 us)
Sparse Core Ops, SparseCore 0:
  10.4 45.1 all-gather.5
  57.9 43.0 all-gather.7
  103.2 122.3 all-gather.9
  227.6 119.6 all-gather.11
  349.3 119.6 all-gather.13
  556.1 73.7 reduce-scatter.8
  634.4 89.0 reduce-scatter.12
  727.8 319.4 reduce-scatter.10
  1051.5 606.2 reduce-scatter.14
  1661.5 94.5 all-reduce.11
where the time goes:
time: 1780 us
  waiting for transfers between devices  1260 us (71%)
  matrix products  199 us (11%)
  blocking collectives  147 us (8%)
  other arithmetic  91.3 us (5%)
  local copies, waits for them, and re-layouts  64.4 us (4%)
    unnamed x12, waiting for transfers between devices  627 us
    reduce_scatter x1, waiting for transfers between devices, on_device(): lax.psum_scatter(down_term(jnp.int32(0), lax.axis_size('fsdp') * (FF // f...  322 us
    all_gather x1, waiting for transfers between devices, on_device(): lax.all_gather(w_up, 'fsdp', axis=0, tiled=True)  106 us
    all_gather x1, waiting for transfers between devices, on_device(): lax.all_gather(w_down, 'fsdp', axis=0, tiled=True)  100 us
    all_gather x1, waiting for transfers between devices, on_device(): lax.all_gather(w_gate, 'fsdp', axis=0, tiled=True)  72 us
    dot_general x7, matrix products, matmul_back(): lax.dot_general(left, right, (((1,), (1,)), ((), ())), preferred_element_...  67.2 us
    dot_general x7, matrix products, term(): lax.dot_general(left, right, (((0,), (0,)), ((), ())), preferred_element_...  64.9 us
    unnamed x1, blocking collectives  63.6 us
  transfers between devices with their start and end apart: 10, of which 7 were waited for; matrix products, arithmetic and copies ran while one was open for 13% of the time, Pallas kernels for 0%

commit v1 on v0

v1 whole, which is shorter than its diff:
```python
import jax
import jax.numpy as jnp
from jax import lax
from jax.sharding import PartitionSpec as P

D = 1152
H = 4
HD = 256
FF = 6912
PIECE = 256

epsilon = 1e-06
rope_base = 1000000.0
masked_value = -1e30
f32 = jnp.float32
bf16 = jnp.bfloat16


def row_scale(values):
    return lax.rsqrt(jnp.mean(values * values, axis=-1, keepdims=True) + epsilon)


def norm_back(values, scale, gain, upstream):
    weighted = upstream * gain
    inner = jnp.mean(weighted * values, axis=-1, keepdims=True)
    grad_values = scale * weighted - values * (scale * scale * scale) * inner
    grad_gain = jnp.sum((upstream * values * scale).reshape(-1, values.shape[-1]), axis=0)
    return (grad_values, grad_gain)


def rope_tables(length, width):
    positions = jnp.arange(length, dtype=f32)
    freqs = rope_base ** (-jnp.arange(width // 2, dtype=f32) * 2.0 / width)
    angles = positions[:, None] * freqs[None, :]
    return (jnp.cos(angles), jnp.sin(angles))


def rotate(values, cosine, sine):
    half = values.shape[-1] // 2
    first = values[..., :half]
    second = values[..., half:]
    return jnp.concatenate(
        [first * cosine - second * sine, second * cosine + first * sine], axis=-1
    )


def rotate_back(upstream, cosine, sine):
    half = upstream.shape[-1] // 2
    first = upstream[..., :half]
    second = upstream[..., half:]
    return jnp.concatenate(
        [first * cosine + second * sine, second * cosine - first * sine], axis=-1
    )


def matmul(left, right):
    return jnp.dot(left, right, preferred_element_type=f32)


def matmul_back(left, right):
    return lax.dot_general(left, right, (((1,), (1,)), ((), ())), preferred_element_type=f32)


def matmul_grad(left, right):
    return lax.dot_general(left, right, (((0,), (0,)), ((), ())), preferred_element_type=f32)


def plane_dims(chips):
    return {8: (4, 2), 32: (8, 4)}.get(chips, (chips, 1))


class Group:
    def __init__(self, count):
        self.count = count
        self.nz, self.ny = plane_dims(count // 2)
        me = lax.axis_index("fsdp")
        self.r = lax.axis_index("replica")
        self.c = me % 2
        self.y = (me // 2) % self.ny
        self.z = me // (2 * self.ny)

    def move(self, value, dz, dy):
        pairs = []
        for z in range(self.nz):
            for y in range(self.ny):
                for c in range(2):
                    to = ((z + dz) % self.nz * self.ny + (y + dy) % self.ny) * 2 + c
                    pairs.append(((z * self.ny + y) * 2 + c, to))
        return lax.ppermute(value, "fsdp", pairs)

    def other_core(self, value):
        return lax.ppermute(value, "fsdp", [(i, i ^ 1) for i in range(self.count)])

    def other_replica(self, value):
        return lax.ppermute(value, "replica", [(0, 1), (1, 0)])

    def gather(self, block):
        buffer = jnp.zeros((self.nz, self.ny) + block.shape, block.dtype)
        for dz in range(self.nz):
            piece = block if dz == 0 else self.move(block, dz, 0)
            for dy in range(self.ny):
                part = piece if dy == 0 else self.move(piece, 0, dy)
                where = ((self.z - dz) % self.nz, (self.y - dy) % self.ny)
                buffer = lax.dynamic_update_slice(
                    buffer, part[None, None], where + (0,) * block.ndim
                )
        return buffer

    def scatter(self, blocks):
        def pick(dz, dy):
            where = ((self.z + dz) % self.nz, (self.y + dy) % self.ny)
            size = (1, 1) + blocks.shape[2:]
            return lax.dynamic_slice(blocks, where + (0,) * (blocks.ndim - 2), size)[0, 0]

        total = None
        for dz in list(range(1, self.nz)) + [0]:
            line = pick(dz, 0).astype(f32)
            for dy in range(1, self.ny):
                line = line + self.move(pick(dz, dy), 0, dy).astype(f32)
            if dz:
                line = self.move(line.astype(bf16), dz, 0).astype(f32)
            total = line if total is None else total + line
        return total

    def by_core(self, mine, theirs):
        first = jnp.where(self.c == 0, mine, theirs)
        second = jnp.where(self.c == 0, theirs, mine)
        return jnp.stack([first, second])

    def by_replica(self, mine, theirs):
        first = jnp.where(self.r == 0, mine, theirs)
        second = jnp.where(self.r == 0, theirs, mine)
        return jnp.stack([first, second])

    def share(self, rows):
        pair = jnp.concatenate([rows, self.other_replica(rows)], axis=0)
        return jnp.concatenate([pair, self.other_core(pair)], axis=0)

    def collect(self, partial):
        half = partial.shape[0] // 2
        pair = partial[:half] + self.other_core(partial[half:].astype(bf16)).astype(f32)
        quarter = half // 2
        return pair[:quarter] + self.other_replica(pair[quarter:].astype(bf16)).astype(f32)


def on_device(
    tokens,
    cotangent,
    piece_starts,
    w_query,
    w_key,
    w_value,
    w_out,
    w_gate,
    w_up,
    w_down,
    attn_pre_gain,
    query_gain,
    key_gain,
    attn_post_gain,
    mlp_pre_gain,
    mlp_post_gain,
):
    length = tokens.shape[0]
    count = lax.axis_size("fsdp")
    group = Group(count)
    chips = count // 2
    d_rows = D // count
    g_rows = HD // count
    o_rows = H * HD // count
    sub = FF // count // 2
    quarter = chips * sub
    qwidth = H * HD
    inner = qwidth + 2 * HD

    gain_block = jnp.zeros((d_rows, 128), bf16)
    for column, gain in enumerate(
        (attn_pre_gain, attn_post_gain, mlp_pre_gain, mlp_post_gain, query_gain, key_gain)
    ):
        gain_block = lax.dynamic_update_slice(gain_block, gain[:, None], (0, column))
    attn_block = jnp.concatenate([w_query, w_key, w_value, gain_block], axis=1)
    attn_core = group.gather(attn_block)
    attn_pairs = group.by_core(attn_core, group.other_core(attn_core))
    attn_all = attn_pairs.transpose(1, 2, 0, 3, 4).reshape(D, inner + 128)
    out_core = group.gather(w_out)
    out_pairs = group.by_core(out_core, group.other_core(out_core))
    w_out_all = out_pairs.transpose(1, 2, 0, 3, 4).reshape(qwidth, D)
    w_qkv = attn_all[:, :inner]
    gains = attn_all[:, inner : inner + 8].astype(f32).T
    gain_attn_pre, gain_attn_post, gain_mlp_pre, gain_mlp_post = (gains[i] for i in range(4))
    head_gains = gains[4:6].reshape(2, count, d_rows)[:, :, :g_rows].reshape(2, HD)
    gain_query, gain_key = head_gains[0], head_gains[1]

    def column_quarter(weight):
        pieces = weight.reshape(d_rows, chips, 2, 2, sub)

        def take(core):
            piece = lax.dynamic_slice(
                pieces, (0, 0, core, group.r, 0), (d_rows, chips, 1, 1, sub)
            )
            return piece.reshape(d_rows, quarter)

        mine = take(group.c)
        return group.by_core(mine, group.other_core(take(1 - group.c)))

    w_gate_q = group.gather(column_quarter(w_gate)).reshape(D, quarter)
    w_up_q = group.gather(column_quarter(w_up)).reshape(D, quarter)
    down_half = lax.dynamic_slice(w_down, (group.r * sub, 0), (sub, D))
    w_down_q = group.gather(down_half).reshape(quarter, D)

    inputs = tokens.astype(f32)
    scale_attn = row_scale(inputs)
    normed_attn = (inputs * scale_attn * gain_attn_pre).astype(bf16)
    projected = matmul(normed_attn, w_qkv)
    query_proj = projected[:, :qwidth].reshape(length, H, HD)
    key_proj = projected[:, qwidth : qwidth + HD]
    value_low = projected[:, qwidth + HD :].astype(bf16)
    cosine, sine = rope_tables(length, HD)
    attn_factor = HD ** (-0.5)
    scale_query = row_scale(query_proj)
    query_low = (
        rotate(query_proj * scale_query * gain_query, cosine[:, None, :], sine[:, None, :])
        * attn_factor
    ).astype(bf16)
    scale_key = row_scale(key_proj)
    key_low = rotate(key_proj * scale_key * gain_key, cosine, sine).astype(bf16)
    rows = jnp.arange(length, dtype=jnp.int32)
    allowed = rows[None, :] <= rows[:, None]
    for piece in range(piece_starts.shape[1]):
        start = piece_starts[0, piece]
        inside = (rows >= start) & (rows < start + PIECE)
        allowed = allowed | (inside[:, None] & inside[None, :])
    scores = jnp.einsum("thd,sd->hts", query_low, key_low, preferred_element_type=f32)
    scores = jnp.where(allowed[None], scores, masked_value)
    peak = jnp.max(scores, axis=-1, keepdims=True)
    expo = jnp.exp(scores - peak)
    total = jnp.sum(expo, axis=-1, keepdims=True)
    probs = expo / total
    probs_low = probs.astype(bf16)
    mixed = jnp.einsum("hts,sd->thd", probs_low, value_low, preferred_element_type=f32)
    mixed_low = mixed.reshape(length, qwidth).astype(bf16)
    attn_out = matmul(mixed_low, w_out_all)
    scale_post = row_scale(attn_out)
    resid = inputs + attn_out * scale_post * gain_attn_post

    scale_mlp = row_scale(resid)
    normed_mlp = (resid * scale_mlp * gain_mlp_pre).astype(bf16)
    normed_all = group.share(normed_mlp)
    gate = matmul(normed_all, w_gate_q)
    upper = matmul(normed_all, w_up_q)
    activated, gelu_pull = jax.vjp(lambda values: jax.nn.gelu(values, approximate=True), gate)
    hidden_low = (activated * upper).astype(bf16)
    mlp_out = group.collect(matmul(hidden_low, w_down_q))
    scale_out = row_scale(mlp_out)
    layer_out = (resid + mlp_out * scale_out * gain_mlp_post).astype(bf16)

    upstream = cotangent.astype(f32)
    grad_mlp_out, grad_mlp_post = norm_back(mlp_out, scale_out, gain_mlp_post, upstream)
    grad_mlp_all = group.share(grad_mlp_out.astype(bf16))
    grad_hidden = matmul_back(grad_mlp_all, w_down_q)
    grad_gate_low = gelu_pull(grad_hidden * upper)[0].astype(bf16)
    grad_up_low = (grad_hidden * activated).astype(bf16)
    down_share = group.scatter(
        matmul_grad(hidden_low, grad_mlp_all)
        .astype(bf16)
        .reshape(group.nz, group.ny, sub, D)
    )
    grad_normed_mlp = group.collect(
        matmul_back(grad_gate_low, w_gate_q) + matmul_back(grad_up_low, w_up_q)
    )

    def column_share(grads):
        share = group.scatter(
            matmul_grad(normed_all, grads)
            .astype(bf16)
            .reshape(group.nz, group.ny, 2, d_rows, quarter)
        ).astype(bf16)
        mine = lax.dynamic_index_in_dim(share, group.c, 0, keepdims=False)
        theirs = lax.dynamic_index_in_dim(share, 1 - group.c, 0, keepdims=False)
        cores = group.by_core(mine, group.other_core(theirs))
        both = group.by_replica(cores, group.other_replica(cores))
        pieces = both.reshape(2, 2, d_rows, chips, sub).transpose(2, 3, 1, 0, 4)
        return pieces.reshape(d_rows, FF).astype(f32)

    grad_gate = column_share(grad_gate_low)
    grad_up = column_share(grad_up_low)
    down_low = down_share.astype(bf16)
    grad_down = (
        group.by_replica(down_low, group.other_replica(down_low)).reshape(2 * sub, D).astype(f32)
    )

    grad_resid_part, grad_mlp_pre = norm_back(resid, scale_mlp, gain_mlp_pre, grad_normed_mlp)
    grad_resid = upstream + grad_resid_part
    grad_attn_out, grad_attn_post = norm_back(attn_out, scale_post, gain_attn_post, grad_resid)
    grad_attn_low = grad_attn_out.astype(bf16)

    def both_sum(terms, rows_each):
        blocks = terms.astype(bf16).reshape(group.nz, group.ny, 2, rows_each, -1)
        mine = lax.dynamic_index_in_dim(blocks, group.c, 2, keepdims=False)
        theirs = lax.dynamic_index_in_dim(blocks, 1 - group.c, 2, keepdims=False)
        blocks = (mine.astype(f32) + group.other_core(theirs).astype(f32)).astype(bf16)
        share = group.scatter(blocks).astype(bf16)
        return share.astype(f32) + group.other_replica(share).astype(f32)

    grad_out = both_sum(matmul_grad(mixed_low, grad_attn_low), o_rows)
    grad_mixed = matmul_back(grad_attn_low, w_out_all).astype(bf16).reshape(length, H, HD)
    grad_probs = jnp.einsum("thd,sd->hts", grad_mixed, value_low, preferred_element_type=f32)
    grad_value_act = jnp.einsum(
        "hts,thd->sd", probs_low, grad_mixed, preferred_element_type=f32
    )
    inner_sum = jnp.sum(probs * grad_probs, axis=-1, keepdims=True)
    grad_scores = (probs * (grad_probs - inner_sum)).astype(bf16)
    grad_query_act = jnp.einsum("hts,sd->thd", grad_scores, key_low, preferred_element_type=f32)
    grad_key_rot = jnp.einsum("hts,thd->sd", grad_scores, query_low, preferred_element_type=f32)
    grad_query_normed = rotate_back(
        grad_query_act * attn_factor, cosine[:, None, :], sine[:, None, :]
    )
    grad_query_proj, grad_query_gain = norm_back(
        query_proj, scale_query, gain_query, grad_query_normed
    )
    grad_key_normed = rotate_back(grad_key_rot, cosine, sine)
    grad_key_proj, grad_key_gain = norm_back(key_proj, scale_key, gain_key, grad_key_normed)
    grad_qkv_low = jnp.concatenate(
        [grad_query_proj.reshape(length, qwidth), grad_key_proj, grad_value_act], axis=1
    ).astype(bf16)
    grad_normed_attn = matmul_back(grad_qkv_low, w_qkv)
    grad_input_part, grad_attn_pre = norm_back(inputs, scale_attn, gain_attn_pre, grad_normed_attn)
    input_grad = grad_resid + grad_input_part
    head_columns = jnp.stack([grad_query_gain, grad_key_gain], axis=1).reshape(count, g_rows, 2)
    head_columns = jnp.pad(head_columns, ((0, 0), (0, d_rows - g_rows), (0, 0))).reshape(D, 2)
    gain_columns = jnp.concatenate(
        [
            jnp.stack([grad_attn_pre, grad_attn_post, grad_mlp_pre, grad_mlp_post], axis=1),
            head_columns,
            jnp.zeros((D, 122), f32),
        ],
        axis=1,
    )
    attn_sum = both_sum(
        jnp.concatenate([matmul_grad(normed_attn, grad_qkv_low), gain_columns], axis=1), d_rows
    )
    gain_sum = attn_sum[:, inner : inner + 8].T
    return (
        layer_out,
        input_grad,
        attn_sum[:, :qwidth],
        attn_sum[:, qwidth : qwidth + HD],
        attn_sum[:, qwidth + HD : inner],
        grad_out,
        grad_gate,
        grad_up,
        grad_down,
        gain_sum[0],
        gain_sum[4, :g_rows],
        gain_sum[5, :g_rows],
        gain_sum[1],
        gain_sum[2],
        gain_sum[3],
    )


def solution(mesh):
    rows = P(("replica", "fsdp"), None)
    weight = P("fsdp", None)
    gain = P("fsdp")
    return jax.shard_map(
        on_device,
        mesh=mesh,
        in_specs=(rows,) * 3 + (weight,) * 7 + (gain,) * 6,
        out_specs=(rows,) * 2 + (weight,) * 7 + (gain,) * 6,
        check_vma=False,
    )
```

time: 1780 us -> 928 us (0.52)
  waiting for transfers between devices: 1260 us -> 378 us
  blocking collectives: 147 us -> 0 us
  starting transfers between devices: 0.57 us -> 132 us
  local copies, waits for them, and re-layouts: 64.4 us -> 167 us
  other arithmetic: 91.3 us -> 63 us
  matrix products: 199 us -> 175 us
    unnamed x12 -> x0, waiting for transfers between devices: 627 us -> none
    ppermute x0 -> x91, waiting for transfers between devices: none -> 378 us  [the longest x70 264 us: move(): return lax.ppermute(value, 'fsdp', pairs)]
    reduce_scatter x2 -> x0, waiting for transfers between devices: 322 us -> none  [the longest x1 322 us: on_device(): lax.psum_scatter(down_term(jnp.int32(0), lax.axis_size('fsdp') * (FF // f...]
    all_gather x5 -> x0, waiting for transfers between devices: 278 us -> none  [the longest x1 106 us: on_device(): lax.all_gather(w_up, 'fsdp', axis=0, tiled=True)]
    ppermute x0 -> x91, starting transfers between devices: none -> 132 us  [the longest x70 118 us: move(): return lax.ppermute(value, 'fsdp', pairs)]
    unnamed x1 -> x0, blocking collectives: 63.6 us -> none
    concatenate x2 -> x3, other arithmetic: 49.6 us -> 2.61 us  [the longest x2 1.89 us: share(): pair = jnp.concatenate([rows, self.other_replica(rows)], axis=0)]
    all_gather x2 -> x0, blocking collectives: 42.4 us -> none  [the longest x1 21.2 us: on_device(): lax.all_gather(w_key, 'fsdp', axis=0, tiled=True)]
  transfers between devices with their start and end apart: 10 -> 91, of which waited for: 7 -> 44; matrix products, arithmetic and copies ran while one was open for 13% -> 30% of each run, Pallas kernels for 0% -> 0%
where the time goes in v1:
time: 928 us; the launch traced here: 918 us
  waiting for transfers between devices  378 us (41%)
  matrix products  175 us (19%)
  local copies, waits for them, and re-layouts  167 us (18%)
  starting transfers between devices  132 us (14%)
  other arithmetic  63 us (7%)
    ppermute x70, waiting for transfers between devices, move(): return lax.ppermute(value, 'fsdp', pairs)  264 us
    ppermute x70, starting transfers between devices, move(): return lax.ppermute(value, 'fsdp', pairs)  118 us
    ppermute x9, waiting for transfers between devices, other_replica(): return lax.ppermute(value, 'replica', [(0, 1), (1, 0)])  108 us
    dot_general x5, matrix products, matmul_back(): lax.dot_general(left, right, (((1,), (1,)), ((), ())), preferred_element_...  63.2 us
    dot_general x5, matrix products, matmul(): return jnp.dot(left, right, preferred_element_type=f32)  55.2 us
    dot_general x5, matrix products, matmul_grad(): lax.dot_general(left, right, (((0,), (0,)), ((), ())), preferred_element_...  41.4 us
    dynamic_update_slice x37, local copies, waits for them, and re-layouts, gather(): lax.dynamic_update_slice(buffer, part[None, None], where + (0,) * block.n...  30.9 us
  transfers between devices with their start and end apart: 91, of which 44 were waited for; matrix products, arithmetic and copies ran while one was open for 30% of the time, Pallas kernels for 0%

profile of v1, /device:TPU:0, one launch (start us, length us, event | category | flops | bytes accessed | tf_op | source)
XLA Modules:
  0.0 918.0 jit_solution(7769870440149426016)
XLA Ops:
  11.6 4.6 reshape.412
  16.3 4.6 reshape.416
  27.2 10.0 %dynamic-slice_reduce_fusion.1 = (bf16[72,8,216]{2,1,0:T(8,128)(2,1)}, bf16[72,8,216]{2,1,0:T(8,128)(2,1)}, bf16[72,8,216]{2,1,0:T(8,128)(2,1)}, bf16[72,8,216]{2,1,0:T(8,128)(2,1)S(1)}) fusion(bf16[72,8,2,2,216]{4,3,2,1,0:T(2,128)(2,1)} %reshape.416, s32[]{:T(128)S(6)} %select_n.686, s32[]{:T(128)S(6)} %select_n.687, s32[]{:T(128)S(6)} %select_n.688, ...), kind=kLoop, calls=%fused_computation.159 | loop fusion | bytes 1990668 | tf_op jit(solution)/shard_map/dynamic_slice | solution.py:198
  51.1 4.1 collective-permute-done
  57.9 5.6 collective-permute-done.1
  69.2 3.8 collective-permute-done.10
  91.3 5.1 collective-permute-done.5
  100.0 6.1 collective-permute-done.6
  111.3 6.8 collective-permute-done.27
  118.6 4.7 collective-permute-done.28
  125.2 4.6 collective-permute-done.19
  130.3 13.6 %collective-permute-done.20 = bf16[2,72,1728]{2,1,0:T(8,128)(2,1)} collective-permute-done((bf16[2,72,1728]{2,1,0:T(8,128)(2,1)S(1)}, bf16[2,72,1728]{2,1,0:T(8,128)(2,1)}, u32[]{:S(2)}, u32[]{:S(2)}) %collective-permute-start.20) | collective-permute-done | bytes 497696 | tf_op jit(solution)/shard_map/ppermute | solution.py:89
  143.8 6.3 collective-permute-start.32
  151.2 18.5 %collective-permute-start.22 = (bf16[2,72,1728]{2,1,0:T(8,128)(2,1)S(1)}, bf16[2,72,1728]{2,1,0:T(8,128)(2,1)}, u32[]{:S(2)}, u32[]{:S(2)}) collective-permute-start(bf16[2,72,1728]{2,1,0:T(8,128)(2,1)S(1)} %pad_maximum_fusion.14), channel_id=1, source_target_pairs={{0,8},{1,9},{2,10},{3,11},{4,12},{5,13},{6,14},{7,15},{8,0},{9,1},... | collective-permute-start | bytes 1493000 | tf_op jit(solution)/shard_map/ppermute | solution.py:89
  174.4 9.8 %collective-permute-done.38 = bf16[216,1152]{1,0:T(8,128)(2,1)S(1)} collective-permute-done((bf16[216,1152]{1,0:T(8,128)(2,1)}, bf16[216,1152]{1,0:T(8,128)(2,1)S(1)}, u32[]{:S(2)}, u32[]{:S(2)}) %collective-permute-start.38) | collective-permute-done | bytes 497696 | tf_op jit(solution)/shard_map/ppermute | solution.py:89
  186.3 8.5 collective-permute-done.40
  195.7 8.9 collective-permute-done.29
  213.9 5.0 collective-permute-done.24
  244.2 5.1 fusion.109
  263.1 20.7 %collective-permute-done.16 = bf16[512,1152]{1,0:T(8,128)(2,1)S(1)} collective-permute-done((bf16[512,1152]{1,0:T(8,128)(2,1)S(1)}, bf16[512,1152]{1,0:T(8,128)(2,1)S(1)}, u32[]{:S(2)}, u32[]{:S(2)}) %collective-permute-start.16) | collective-permute-done | bytes 1179680 | tf_op jit(solution)/shard_map/ppermute | solution.py:95
  290.5 14.9 %fusion.107 = f32[2048,1728]{0,1:T(8,128)} fusion(bf16[1152,1728]{1,0:T(8,128)(2,1)S(1)} %bitcast.403, bf16[1024,1152]{1,0:T(8,128)(2,1)S(1)} %collective-permute-done.17, bf16[512,1152]{1,0:T(8,128)(2,1)S(1)} %collective-permute-done.16, bf16[512,1152]{1,0:T(8,128)(2,1)S(1)} %multiply_convert_fusion.2), kind=kOutput, calls=%fused_computation.332 | convolution fusion | flops 8167882752 | bytes 22855680 | tf_op jit(solution)/shard_map/dot_general | solution.py:57
  305.4 22.5 %multiply_convert_fusion.1 = (bf16[2048,1728]{0,1:T(8,128)(2,1)}, f32[2048,1728]{0,1:T(8,128)}) fusion(f32[2048,1728]{0,1:T(8,128)} %fusion.107, bf16[1152,1728]{1,0:T(8,128)(2,1)} %bitcast.401, bf16[1024,1152]{1,0:T(8,128)(2,1)} %copy-done.114, bf16[512,1152]{1,0:T(8,128)(2,1)} %copy-done.52, bf16[512,1152]{1,0:T(8,128)(2,1)S(1)} %multiply_convert_fusion.2), kind=kOutput, calls=%fused_computation.11 | convolution fusion | flops 8203272192 | bytes 44089344 | tf_op jit(solution)/shard_map/dot_general | solution.py:57
  327.9 13.9 %fusion.114 = f32[2048,1152]{1,0:T(8,128)S(1)} fusion(bf16[2048,1728]{0,1:T(8,128)(2,1)} %get-tuple-element.135, bf16[1728,1152]{1,0:T(8,128)(2,1)} %bitcast.71), kind=kOutput, calls=%fused_computation.335 | convolution fusion | flops 8153726976 | bytes 20496384 | tf_op jit(solution)/shard_map/dot_general | solution.py:57
  342.4 4.2 collective-permute-done.41
  348.7 26.7 %collective-permute-done.42 = bf16[512,1152]{1,0:T(8,128)(2,1)S(1)} collective-permute-done((bf16[512,1152]{1,0:T(8,128)(2,1)S(1)}, bf16[512,1152]{1,0:T(8,128)(2,1)S(1)}, u32[]{:S(2)}, u32[]{:S(2)}) %collective-permute-start.42) | collective-permute-done | bytes 1179680 | tf_op jit(solution)/shard_map/ppermute | solution.py:95
  380.4 25.9 %collective-permute-done.43 = bf16[512,1152]{1,0:T(8,128)(2,1)S(1)} collective-permute-done((bf16[512,1152]{1,0:T(8,128)(2,1)S(1)}, bf16[512,1152]{1,0:T(8,128)(2,1)S(1)}, u32[]{:S(2)}, u32[]{:S(2)}) %collective-permute-start.43) | collective-permute-done | bytes 1179680 | tf_op jit(solution)/shard_map/ppermute | solution.py:95
  417.4 12.6 %convolution_convert_fusion.3 = bf16[1728,1152]{1,0:T(8,128)(2,1)S(1)} fusion(bf16[2048,1728]{0,1:T(8,128)(2,1)} %get-tuple-element.135, bf16[1024,1152]{1,0:T(8,128)(2,1)} %collective-permute-done.44, bf16[512,1152]{1,0:T(8,128)(2,1)S(1)} %copy-done.55, bf16[512,1152]{1,0:T(8,128)(2,1)S(1)} %copy-done.29), kind=kOutput, calls=%fused_computation.17 | convolution fusion | flops 8169873408 | bytes 15777792 | tf_op jit(solution)/shard_map/dot_general | solution.py:65
  435.6 27.6 %fusion.7 = (bf16[2048,1728]{0,1:T(8,128)(2,1)}, bf16[2048,1728]{0,1:T(8,128)(2,1)S(1)}) fusion(f32[2048,1728]{0,1:T(8,128)} %fusion.107, f32[2048,1728]{0,1:T(8,128)} %get-tuple-element.136, bf16[1728,1152]{1,0:T(8,128)(2,1)} %bitcast.71, bf16[1024,1152]{1,0:T(8,128)(2,1)} %collective-permute-done.44, bf16[512,1152]{1,0:T(8,128)(2,1)S(1)} %copy-done.55, ...), kind=kOutput, calls=%fused_computation.9 | convolution fusion | flops 8252817408 | bytes 51167232 | tf_op jit(solution)/shard_map/dot_general | solution.py:61
  463.2 12.5 %fusion.115 = f32[2048,1152]{1,0:T(8,128)} fusion(bf16[2048,1728]{0,1:T(8,128)(2,1)S(1)} %get-tuple-element.47, bf16[1152,1728]{1,0:T(8,128)(2,1)S(1)} %bitcast.402), kind=kOutput, calls=%fused_computation.336 | convolution fusion | flops 8153726976 | bytes 20496384 | tf_op jit(solution)/shard_map/dot_general | solution.py:61
  475.7 10.8 %convolution_convert_fusion.1 = bf16[1152,1728]{0,1:T(8,128)(2,1)} fusion(bf16[2048,1728]{0,1:T(8,128)(2,1)S(1)} %get-tuple-element.47, bf16[1024,1152]{1,0:T(8,128)(2,1)S(1)} %copy-done.115, bf16[512,1152]{1,0:T(8,128)(2,1)S(1)} %copy-done.53, bf16[512,1152]{1,0:T(8,128)(2,1)S(1)} %multiply_convert_fusion.2), kind=kOutput, calls=%fused_computation.15 | convolution fusion | flops 8169873408 | bytes 15777792 | tf_op jit(solution)/shard_map/dot_general | solution.py:65
  486.5 6.4 copy.262
  496.1 16.1 %convolution_add_fusion = f32[2048,1152]{1,0:T(8,128)} fusion(f32[2048,1152]{1,0:T(8,128)} %fusion.115, bf16[2048,1728]{0,1:T(8,128)(2,1)} %get-tuple-element.46, bf16[1152,1728]{1,0:T(8,128)(2,1)S(1)} %bitcast.404), kind=kOutput, calls=%fused_computation.13 | convolution fusion | flops 8156086272 | bytes 29933568 | tf_op jit(solution)/shard_map/dot_general | solution.py:61
  512.3 11.0 %convolution_convert_fusion.2 = bf16[1152,1728]{0,1:T(8,128)(2,1)} fusion(bf16[2048,1728]{0,1:T(8,128)(2,1)S(1)} %bitcast.425, bf16[1024,1152]{1,0:T(8,128)(2,1)S(1)} %copy-done.116, bf16[512,1152]{1,0:T(8,128)(2,1)S(1)} %copy-done.53, bf16[512,1152]{1,0:T(8,128)(2,1)S(1)} %multiply_convert_fusion.2), kind=kOutput, calls=%fused_computation.16 | convolution fusion | flops 8169873408 | bytes 15777792 | tf_op jit(solution)/shard_map/dot_general | solution.py:65
  523.3 6.6 copy.260
  539.6 8.8 collective-permute-done.76
  549.8 9.7 %collective-permute-done.78 = bf16[2,72,1728]{2,1,0:T(8,128)(2,1)S(1)} collective-permute-done((bf16[2,72,1728]{2,1,0:T(8,128)(2,1)S(1)}, bf16[2,72,1728]{2,1,0:T(8,128)(2,1)S(1)}, u32[]{:S(2)}, u32[]{:S(2)}) %collective-permute-start.78) | collective-permute-done | bytes 497696 | tf_op jit(solution)/shard_map/ppermute | solution.py:89
  561.2 20.4 %collective-permute-done.65 = bf16[2,72,1728]{2,1,0:T(8,128)(2,1)S(1)} collective-permute-done((bf16[2,72,1728]{2,1,0:T(8,128)(2,1)S(1)}, bf16[2,72,1728]{2,1,0:T(8,128)(2,1)S(1)}, u32[]{:S(2)}, u32[]{:S(2)}) %collective-permute-start.65) | collective-permute-done | bytes 497696 | tf_op jit(solution)/shard_map/ppermute | solution.py:89
  583.3 9.4 %collective-permute-done.67 = bf16[2,72,1728]{2,1,0:T(8,128)(2,1)S(1)} collective-permute-done((bf16[2,72,1728]{2,1,0:T(8,128)(2,1)S(1)}, bf16[2,72,1728]{2,1,0:T(8,128)(2,1)S(1)}, u32[]{:S(2)}, u32[]{:S(2)}) %collective-permute-start.67) | collective-permute-done | bytes 497696 | tf_op jit(solution)/shard_map/ppermute | solution.py:89
  593.2 8.8 collective-permute-done.69
  602.0 3.3 collective-permute-start.79
  606.9 11.1 %collective-permute-done.77 = bf16[2,72,1728]{2,1,0:T(8,128)(2,1)S(1)} collective-permute-done((bf16[2,72,1728]{2,1,0:T(8,128)(2,1)S(1)}, bf16[2,72,1728]{2,1,0:T(8,128)(2,1)S(1)}, u32[]{:S(2)}, u32[]{:S(2)}) %collective-permute-start.77) | collective-permute-done | bytes 497696 | tf_op jit(solution)/shard_map/ppermute | solution.py:89
  618.0 17.4 %collective-permute-done.79 = bf16[2,72,1728]{2,1,0:T(8,128)(2,1)S(1)} collective-permute-done((bf16[2,72,1728]{2,1,0:T(8,128)(2,1)S(1)}, bf16[2,72,1728]{2,1,0:T(8,128)(2,1)S(1)}, u32[]{:S(2)}, u32[]{:S(2)}) %collective-permute-start.79) | collective-permute-done | bytes 497696 | tf_op jit(solution)/shard_map/ppermute | solution.py:89
  635.9 22.0 %collective-permute-start.66 = (bf16[2,72,1728]{2,1,0:T(8,128)(2,1)S(1)}, bf16[2,72,1728]{2,1,0:T(8,128)(2,1)S(1)}, u32[]{:S(2)}, u32[]{:S(2)}) collective-permute-start(bf16[2,72,1728]{2,1,0:T(8,128)(2,1)S(1)} %get-tuple-element.57), channel_id=1, source_target_pairs={{0,4},{1,5},{2,6},{3,7},{4,8},{5,9},{6,10},{7,11},{8,12},{9,13},{1... | collective-permute-start | bytes 1493000 | tf_op jit(solution)/shard_map/ppermute | solution.py:89
  659.9 20.8 %collective-permute-done.88 = bf16[216,1152]{1,0:T(8,128)(2,1)S(1)} collective-permute-done((bf16[216,1152]{1,0:T(8,128)(2,1)S(1)}, bf16[216,1152]{1,0:T(8,128)(2,1)S(1)}, u32[]{:S(2)}, u32[]{:S(2)}) %collective-permute-start.88) | collective-permute-done | bytes 497696 | tf_op jit(solution)/shard_map/ppermute | solution.py:89
  683.6 19.5 %collective-permute-done.68 = bf16[2,72,1728]{2,1,0:T(8,128)(2,1)S(1)} collective-permute-done((bf16[2,72,1728]{2,1,0:T(8,128)(2,1)S(1)}, bf16[2,72,1728]{2,1,0:T(8,128)(2,1)S(1)}, u32[]{:S(2)}, u32[]{:S(2)}) %collective-permute-start.68) | collective-permute-done | bytes 497696 | tf_op jit(solution)/shard_map/ppermute | solution.py:89
  703.1 10.7 %collective-permute-done.70 = bf16[2,72,1728]{2,1,0:T(8,128)(2,1)S(1)} collective-permute-done((bf16[2,72,1728]{2,1,0:T(8,128)(2,1)S(1)}, bf16[2,72,1728]{2,1,0:T(8,128)(2,1)S(1)}, u32[]{:S(2)}, u32[]{:S(2)}) %collective-permute-start.70) | collective-permute-done | bytes 497696 | tf_op jit(solution)/shard_map/ppermute | solution.py:89
  722.5 6.5 collective-permute-done.82
  732.7 7.4 collective-permute-done.73
  748.9 16.2 %collective-permute-done.46 = bf16[512,1152]{1,0:T(8,128)(2,1)} collective-permute-done((bf16[512,1152]{1,0:T(8,128)(2,1)}, bf16[512,1152]{1,0:T(8,128)(2,1)}, u32[]{:S(2)}, u32[]{:S(2)}) %collective-permute-start.46) | collective-permute-done | bytes 1179680 | tf_op jit(solution)/shard_map/ppermute | solution.py:95
  765.1 3.3 multiply_reduce_fusion
  781.6 3.4 fusion.8
  805.4 4.0 convolution_convert_fusion
  809.4 4.5 fusion.32
  825.0 6.4 concatenate.84
  836.1 3.3 copy.263
  839.4 4.6 reshape.446
  844.0 3.3 copy.261
  847.3 4.6 reshape.441
  852.6 3.8 fusion.29
  872.2 7.5 collective-permute-done.48
  879.7 5.1 collective-permute-done.50
  895.4 5.1 collective-permute-done.49
  900.4 7.9 collective-permute-done.51
  910.8 4.1 collective-permute-done.55
  (592 shorter events, 283.6 us)
Async XLA Ops:
  4.0 102.7 %collective-permute-start.34 = (bf16[216,1152]{1,0:T(8,128)(2,1)}, bf16[216,1152]{1,0:T(8,128)(2,1)}, u32[]{:S(2)}, u32[]{:S(2)}) collective-permute-start(bf16[216,1152]{1,0:T(8,128)(2,1)} %get-tuple-element.43), channel_id=1, source_target_pairs={{0,2},{1,3},{2,0},{3,1},{4,6},{5,7},{6,4},{7,5},{8,10},{9,11},{10,... | collective-permute-start | bytes 1493000 | tf_op jit(solution)/shard_map/ppermute | solution.py:89
  6.9 101.7 %collective-permute-start.35 = (bf16[216,1152]{1,0:T(8,128)(2,1)}, bf16[216,1152]{1,0:T(8,128)(2,1)}, u32[]{:S(2)}, u32[]{:S(2)}) collective-permute-start(bf16[216,1152]{1,0:T(8,128)(2,1)} %get-tuple-element.43), channel_id=1, source_target_pairs={{0,4},{1,5},{2,6},{3,7},{4,8},{5,9},{6,10},{7,11},{8,12},{9,13},{1... | collective-permute-start | bytes 1493000 | tf_op jit(solution)/shard_map/ppermute | solution.py:89
  8.5 142.7 %collective-permute-start.37 = (bf16[216,1152]{1,0:T(8,128)(2,1)}, bf16[216,1152]{1,0:T(8,128)(2,1)}, u32[]{:S(2)}, u32[]{:S(2)}) collective-permute-start(bf16[216,1152]{1,0:T(8,128)(2,1)} %get-tuple-element.43), channel_id=1, source_target_pairs={{0,8},{1,9},{2,10},{3,11},{4,12},{5,13},{6,14},{7,15},{8,0},{9,1},... | collective-permute-start | bytes 1493000 | tf_op jit(solution)/shard_map/ppermute | solution.py:89
  11.1 34.3 %collective-permute-start.8 = (bf16[64,1152]{1,0:T(8,128)(2,1)}, bf16[64,1152]{1,0:T(8,128)(2,1)}, u32[]{:S(2)}, u32[]{:S(2)}) collective-permute-start(bf16[64,1152]{1,0:T(8,128)(2,1)} %param.22), channel_id=1, source_target_pairs={{0,2},{1,3},{2,0},{3,1},{4,6},{5,7},{6,4},{7,5},{8,10},{9,11},{10,... | collective-permute-start | bytes 442376 | tf_op jit(solution)/shard_map/ppermute | solution.py:89
  11.6 37.3 %collective-permute-start.9 = (bf16[64,1152]{1,0:T(8,128)(2,1)}, bf16[64,1152]{1,0:T(8,128)(2,1)S(1)}, u32[]{:S(2)}, u32[]{:S(2)}) collective-permute-start(bf16[64,1152]{1,0:T(8,128)(2,1)} %param.22), channel_id=1, source_target_pairs={{0,4},{1,5},{2,6},{3,7},{4,8},{5,9},{6,10},{7,11},{8,12},{9,13},{1... | collective-permute-start | bytes 442376 | tf_op jit(solution)/shard_map/ppermute | solution.py:89
  45.3 23.7 %collective-permute-start.11 = (bf16[64,1152]{1,0:T(8,128)(2,1)}, bf16[64,1152]{1,0:T(8,128)(2,1)S(1)}, u32[]{:S(2)}, u32[]{:S(2)}) collective-permute-start(bf16[64,1152]{1,0:T(8,128)(2,1)} %param.22), channel_id=1, source_target_pairs={{0,8},{1,9},{2,10},{3,11},{4,12},{5,13},{6,14},{7,15},{8,0},{9,1},... | collective-permute-start | bytes 442376 | tf_op jit(solution)/shard_map/ppermute | solution.py:89
  75.9 12.9 %collective-permute-start.3 = (bf16[72,1664]{1,0:T(8,128)(2,1)S(1)}, bf16[72,1664]{1,0:T(8,128)(2,1)S(1)}, u32[]{:S(2)}, u32[]{:S(2)}) collective-permute-start(bf16[72,1664]{1,0:T(8,128)(2,1)S(1)} %copy-done.72), channel_id=1, source_target_pairs={{0,8},{1,9},{2,10},{3,11},{4,12},{5,13},{6,14},{7,15},{8,0},{9,1},... | collective-permute-start | bytes 718856 | tf_op jit(solution)/shard_map/ppermute | solution.py:89
  96.5 73.2 %collective-permute-start.39 = (bf16[216,1152]{1,0:T(8,128)(2,1)}, bf16[216,1152]{1,0:T(8,128)(2,1)S(1)}, u32[]{:S(2)}, u32[]{:S(2)}) collective-permute-start(bf16[216,1152]{1,0:T(8,128)(2,1)} %get-tuple-element.43), channel_id=1, source_target_pairs={{0,12},{1,13},{2,14},{3,15},{4,0},{5,1},{6,2},{7,3},{8,4},{9,5},{1... | collective-permute-start | bytes 1493000 | tf_op jit(solution)/shard_map/ppermute | solution.py:89
  106.6 16.6 %collective-permute-start.28 = (bf16[2,72,1728]{2,1,0:T(8,128)(2,1)S(1)}, bf16[2,72,1728]{2,1,0:T(8,128)(2,1)S(1)}, u32[]{:S(2)}, u32[]{:S(2)}) collective-permute-start(bf16[2,72,1728]{2,1,0:T(8,128)(2,1)S(1)} %pad_maximum_fusion.15), channel_id=1, source_target_pairs={{0,4},{1,5},{2,6},{3,7},{4,8},{5,9},{6,10},{7,11},{8,12},{9,13},{1... | collective-permute-start | bytes 1493000 | tf_op jit(solution)/shard_map/ppermute | solution.py:89
  108.6 96.1 %collective-permute-start.30 = (bf16[2,72,1728]{2,1,0:T(8,128)(2,1)S(1)}, bf16[2,72,1728]{2,1,0:T(8,128)(2,1)}, u32[]{:S(2)}, u32[]{:S(2)}) collective-permute-start(bf16[2,72,1728]{2,1,0:T(8,128)(2,1)S(1)} %pad_maximum_fusion.15), channel_id=1, source_target_pairs={{0,8},{1,9},{2,10},{3,11},{4,12},{5,13},{6,14},{7,15},{8,0},{9,1},... | collective-permute-start | bytes 1493000 | tf_op jit(solution)/shard_map/ppermute | solution.py:89
  123.3 20.5 %collective-permute-start.20 = (bf16[2,72,1728]{2,1,0:T(8,128)(2,1)S(1)}, bf16[2,72,1728]{2,1,0:T(8,128)(2,1)}, u32[]{:S(2)}, u32[]{:S(2)}) collective-permute-start(bf16[2,72,1728]{2,1,0:T(8,128)(2,1)S(1)} %pad_maximum_fusion.14), channel_id=1, source_target_pairs={{0,4},{1,5},{2,6},{3,7},{4,8},{5,9},{6,10},{7,11},{8,12},{9,13},{1... | collective-permute-start | bytes 1493000 | tf_op jit(solution)/shard_map/ppermute | solution.py:89
  129.8 40.4 %collective-permute-start.36 = (bf16[216,1152]{1,0:T(8,128)(2,1)}, bf16[216,1152]{1,0:T(8,128)(2,1)S(1)}, u32[]{:S(2)}, u32[]{:S(2)}) collective-permute-start(bf16[216,1152]{1,0:T(8,128)(2,1)} %collective-permute-done.35), channel_id=1, source_target_pairs={{0,2},{1,3},{2,0},{3,1},{4,6},{5,7},{6,4},{7,5},{8,10},{9,11},{10,... | collective-permute-start | bytes 1493000 | tf_op jit(solution)/shard_map/ppermute | solution.py:89
  143.8 68.1 %collective-permute-start.32 = (bf16[2,72,1728]{2,1,0:T(8,128)(2,1)S(1)}, bf16[2,72,1728]{2,1,0:T(8,128)(2,1)}, u32[]{:S(2)}, u32[]{:S(2)}) collective-permute-start(bf16[2,72,1728]{2,1,0:T(8,128)(2,1)S(1)} %pad_maximum_fusion.15), channel_id=1, source_target_pairs={{0,12},{1,13},{2,14},{3,15},{4,0},{5,1},{6,2},{7,3},{8,4},{9,5},{1... | collective-permute-start | bytes 1493000 | tf_op jit(solution)/shard_map/ppermute | solution.py:89
  151.2 61.4 %collective-permute-start.22 = (bf16[2,72,1728]{2,1,0:T(8,128)(2,1)S(1)}, bf16[2,72,1728]{2,1,0:T(8,128)(2,1)}, u32[]{:S(2)}, u32[]{:S(2)}) collective-permute-start(bf16[2,72,1728]{2,1,0:T(8,128)(2,1)S(1)} %pad_maximum_fusion.14), channel_id=1, source_target_pairs={{0,8},{1,9},{2,10},{3,11},{4,12},{5,13},{6,14},{7,15},{8,0},{9,1},... | collective-permute-start | bytes 1493000 | tf_op jit(solution)/shard_map/ppermute | solution.py:89
  169.7 14.5 %collective-permute-start.38 = (bf16[216,1152]{1,0:T(8,128)(2,1)}, bf16[216,1152]{1,0:T(8,128)(2,1)S(1)}, u32[]{:S(2)}, u32[]{:S(2)}) collective-permute-start(bf16[216,1152]{1,0:T(8,128)(2,1)} %collective-permute-done.37), channel_id=1, source_target_pairs={{0,2},{1,3},{2,0},{3,1},{4,6},{5,7},{6,4},{7,5},{8,10},{9,11},{10,... | collective-permute-start | bytes 1493000 | tf_op jit(solution)/shard_map/ppermute | solution.py:89
  170.1 24.7 %collective-permute-start.40 = (bf16[216,1152]{1,0:T(8,128)(2,1)S(1)}, bf16[216,1152]{1,0:T(8,128)(2,1)S(1)}, u32[]{:S(2)}, u32[]{:S(2)}) collective-permute-start(bf16[216,1152]{1,0:T(8,128)(2,1)S(1)} %collective-permute-done.39), channel_id=1, source_target_pairs={{0,2},{1,3},{2,0},{3,1},{4,6},{5,7},{6,4},{7,5},{8,10},{9,11},{10,... | collective-permute-start | bytes 1493000 | tf_op jit(solution)/shard_map/ppermute | solution.py:89
  184.2 20.4 %collective-permute-start.29 = (bf16[2,72,1728]{2,1,0:T(8,128)(2,1)S(1)}, bf16[2,72,1728]{2,1,0:T(8,128)(2,1)S(1)}, u32[]{:S(2)}, u32[]{:S(2)}) collective-permute-start(bf16[2,72,1728]{2,1,0:T(8,128)(2,1)S(1)} %collective-permute-done.28), channel_id=1, source_target_pairs={{0,2},{1,3},{2,0},{3,1},{4,6},{5,7},{6,4},{7,5},{8,10},{9,11},{10,... | collective-permute-start | bytes 1493000 | tf_op jit(solution)/shard_map/ppermute | solution.py:89
  204.6 14.8 %collective-permute-start.7 = (bf16[4,2,72,1664]{3,2,1,0:T(8,128)(2,1)S(1)}, bf16[4,2,72,1664]{3,2,1,0:T(8,128)(2,1)S(1)}, u32[]{:S(2)}, u32[]{:S(2)}) collective-permute-start(bf16[4,2,72,1664]{3,2,1,0:T(8,128)(2,1)S(1)} %bitcast_dynamic-update-slice_fusion.24), channel_id=1, source_target_pairs={{0,1},{1,0},{2,3},{3,2},{4,5},{5,4},{6,7},{7,6},{8,9},{9,8},{10,11... | collective-permute-start | bytes 5750792 | tf_op jit(solution)/shard_map/ppermute | solution.py:92
  204.6 14.3 %collective-permute-start.24 = (bf16[2,72,1728]{2,1,0:T(8,128)(2,1)S(1)}, bf16[2,72,1728]{2,1,0:T(8,128)(2,1)}, u32[]{:S(2)}, u32[]{:S(2)}) collective-permute-start(bf16[2,72,1728]{2,1,0:T(8,128)(2,1)S(1)} %pad_maximum_fusion.14), channel_id=1, source_target_pairs={{0,12},{1,13},{2,14},{3,15},{4,0},{5,1},{6,2},{7,3},{8,4},{9,5},{1... | collective-permute-start | bytes 1493000 | tf_op jit(solution)/shard_map/ppermute | solution.py:89
  207.3 49.3 %collective-permute-start.31 = (bf16[2,72,1728]{2,1,0:T(8,128)(2,1)}, bf16[2,72,1728]{2,1,0:T(8,128)(2,1)}, u32[]{:S(2)}, u32[]{:S(2)}) collective-permute-start(bf16[2,72,1728]{2,1,0:T(8,128)(2,1)} %collective-permute-done.30), channel_id=1, source_target_pairs={{0,2},{1,3},{2,0},{3,1},{4,6},{5,7},{6,4},{7,5},{8,10},{9,11},{10,... | collective-permute-start | bytes 1493000 | tf_op jit(solution)/shard_map/ppermute | solution.py:89
  211.9 50.1 %collective-permute-start.21 = (bf16[2,72,1728]{2,1,0:T(8,128)(2,1)}, bf16[2,72,1728]{2,1,0:T(8,128)(2,1)}, u32[]{:S(2)}, u32[]{:S(2)}) collective-permute-start(bf16[2,72,1728]{2,1,0:T(8,128)(2,1)} %collective-permute-done.20), channel_id=1, source_target_pairs={{0,2},{1,3},{2,0},{3,1},{4,6},{5,7},{6,4},{7,5},{8,10},{9,11},{10,... | collective-permute-start | bytes 1493000 | tf_op jit(solution)/shard_map/ppermute | solution.py:89
  212.6 74.8 %collective-permute-start.33 = (bf16[2,72,1728]{2,1,0:T(8,128)(2,1)}, bf16[2,72,1728]{2,1,0:T(8,128)(2,1)}, u32[]{:S(2)}, u32[]{:S(2)}) collective-permute-start(bf16[2,72,1728]{2,1,0:T(8,128)(2,1)} %collective-permute-done.32), channel_id=1, source_target_pairs={{0,2},{1,3},{2,0},{3,1},{4,6},{5,7},{6,4},{7,5},{8,10},{9,11},{10,... | collective-permute-start | bytes 1493000 | tf_op jit(solution)/shard_map/ppermute | solution.py:89
  219.0 66.3 %collective-permute-start.23 = (bf16[2,72,1728]{2,1,0:T(8,128)(2,1)}, bf16[2,72,1728]{2,1,0:T(8,128)(2,1)}, u32[]{:S(2)}, u32[]{:S(2)}) collective-permute-start(bf16[2,72,1728]{2,1,0:T(8,128)(2,1)} %collective-permute-done.22), channel_id=1, source_target_pairs={{0,2},{1,3},{2,0},{3,1},{4,6},{5,7},{6,4},{7,5},{8,10},{9,11},{10,... | collective-permute-start | bytes 1493000 | tf_op jit(solution)/shard_map/ppermute | solution.py:89
  219.4 69.9 %collective-permute-start.25 = (bf16[2,72,1728]{2,1,0:T(8,128)(2,1)}, bf16[2,72,1728]{2,1,0:T(8,128)(2,1)}, u32[]{:S(2)}, u32[]{:S(2)}) collective-permute-start(bf16[2,72,1728]{2,1,0:T(8,128)(2,1)} %collective-permute-done.24), channel_id=1, source_target_pairs={{0,2},{1,3},{2,0},{3,1},{4,6},{5,7},{6,4},{7,5},{8,10},{9,11},{10,... | collective-permute-start | bytes 1493000 | tf_op jit(solution)/shard_map/ppermute | solution.py:89
  256.6 27.1 %collective-permute-start.16 = (bf16[512,1152]{1,0:T(8,128)(2,1)S(1)}, bf16[512,1152]{1,0:T(8,128)(2,1)S(1)}, u32[]{:S(2)}, u32[]{:S(2)}) collective-permute-start(bf16[512,1152]{1,0:T(8,128)(2,1)S(1)} %multiply_convert_fusion.2), channel_id=1, source_target_pairs={{0,16},{16,0},{1,17},{17,1},{2,18},{18,2},{3,19},{19,3},{4,20},{20... | collective-permute-start | bytes 3538952 | tf_op jit(solution)/shard_map/ppermute | solution.py:95
  347.1 28.3 %collective-permute-start.42 = (bf16[512,1152]{1,0:T(8,128)(2,1)S(1)}, bf16[512,1152]{1,0:T(8,128)(2,1)S(1)}, u32[]{:S(2)}, u32[]{:S(2)}) collective-permute-start(bf16[512,1152]{1,0:T(8,128)(2,1)S(1)} %slice.272), channel_id=1, source_target_pairs={{0,16},{16,0},{1,17},{17,1},{2,18},{18,2},{3,19},{19,3},{4,20},{20... | collective-permute-start | bytes 3538952 | tf_op jit(solution)/shard_map/ppermute | solution.py:95
  378.9 27.4 %collective-permute-start.43 = (bf16[512,1152]{1,0:T(8,128)(2,1)S(1)}, bf16[512,1152]{1,0:T(8,128)(2,1)S(1)}, u32[]{:S(2)}, u32[]{:S(2)}) collective-permute-start(bf16[512,1152]{1,0:T(8,128)(2,1)S(1)} %get-tuple-element.48), channel_id=1, source_target_pairs={{0,16},{16,0},{1,17},{17,1},{2,18},{18,2},{3,19},{19,3},{4,20},{20... | collective-permute-start | bytes 3538952 | tf_op jit(solution)/shard_map/ppermute | solution.py:95
  431.5 102.1 %collective-permute-start.83 = (bf16[216,1152]{1,0:T(8,128)(2,1)}, bf16[216,1152]{1,0:T(8,128)(2,1)}, u32[]{:S(2)}, u32[]{:S(2)}) collective-permute-start(bf16[216,1152]{1,0:T(8,128)(2,1)} %get-tuple-element.67), channel_id=1, source_target_pairs={{0,2},{1,3},{2,0},{3,1},{4,6},{5,7},{6,4},{7,5},{8,10},{9,11},{10,... | collective-permute-start | bytes 1493000 | tf_op jit(solution)/shard_map/ppermute | solution.py:89
  432.0 103.1 %collective-permute-start.85 = (bf16[216,1152]{1,0:T(8,128)(2,1)}, bf16[216,1152]{1,0:T(8,128)(2,1)}, u32[]{:S(2)}, u32[]{:S(2)}) collective-permute-start(bf16[216,1152]{1,0:T(8,128)(2,1)} %get-tuple-element.70), channel_id=1, source_target_pairs={{0,2},{1,3},{2,0},{3,1},{4,6},{5,7},{6,4},{7,5},{8,10},{9,11},{10,... | collective-permute-start | bytes 1493000 | tf_op jit(solution)/shard_map/ppermute | solution.py:89
  433.6 102.1 %collective-permute-start.87 = (bf16[216,1152]{1,0:T(8,128)(2,1)}, bf16[216,1152]{1,0:T(8,128)(2,1)}, u32[]{:S(2)}, u32[]{:S(2)}) collective-permute-start(bf16[216,1152]{1,0:T(8,128)(2,1)} %get-tuple-element.69), channel_id=1, source_target_pairs={{0,2},{1,3},{2,0},{3,1},{4,6},{5,7},{6,4},{7,5},{8,10},{9,11},{10,... | collective-permute-start | bytes 1493000 | tf_op jit(solution)/shard_map/ppermute | solution.py:89
  434.0 201.8 %collective-permute-start.89 = (bf16[216,1152]{1,0:T(8,128)(2,1)}, bf16[216,1152]{1,0:T(8,128)(2,1)}, u32[]{:S(2)}, u32[]{:S(2)}) collective-permute-start(bf16[216,1152]{1,0:T(8,128)(2,1)} %get-tuple-element.68), channel_id=1, source_target_pairs={{0,2},{1,3},{2,0},{3,1},{4,6},{5,7},{6,4},{7,5},{8,10},{9,11},{10,... | collective-permute-start | bytes 1493000 | tf_op jit(solution)/shard_map/ppermute | solution.py:89
  495.7 43.1 %collective-permute-start.74 = (bf16[2,72,1728]{2,1,0:T(8,128)(2,1)}, bf16[2,72,1728]{2,1,0:T(8,128)(2,1)S(1)}, u32[]{:S(2)}, u32[]{:S(2)}) collective-permute-start(bf16[2,72,1728]{2,1,0:T(8,128)(2,1)} %get-tuple-element.53), channel_id=1, source_target_pairs={{0,2},{1,3},{2,0},{3,1},{4,6},{5,7},{6,4},{7,5},{8,10},{9,11},{10,... | collective-permute-start | bytes 1493000 | tf_op jit(solution)/shard_map/ppermute | solution.py:89
  533.6 14.8 %collective-permute-start.76 = (bf16[2,72,1728]{2,1,0:T(8,128)(2,1)S(1)}, bf16[2,72,1728]{2,1,0:T(8,128)(2,1)S(1)}, u32[]{:S(2)}, u32[]{:S(2)}) collective-permute-start(bf16[2,72,1728]{2,1,0:T(8,128)(2,1)S(1)} %copy-done.70), channel_id=1, source_target_pairs={{0,2},{1,3},{2,0},{3,1},{4,6},{5,7},{6,4},{7,5},{8,10},{9,11},{10,... | collective-permute-start | bytes 1493000 | tf_op jit(solution)/shard_map/ppermute | solution.py:89
  535.1 24.4 %collective-permute-start.78 = (bf16[2,72,1728]{2,1,0:T(8,128)(2,1)S(1)}, bf16[2,72,1728]{2,1,0:T(8,128)(2,1)S(1)}, u32[]{:S(2)}, u32[]{:S(2)}) collective-permute-start(bf16[2,72,1728]{2,1,0:T(8,128)(2,1)S(1)} %copy-done.69), channel_id=1, source_target_pairs={{0,2},{1,3},{2,0},{3,1},{4,6},{5,7},{6,4},{7,5},{8,10},{9,11},{10,... | collective-permute-start | bytes 1493000 | tf_op jit(solution)/shard_map/ppermute | solution.py:89
  535.7 70.0 %collective-permute-start.80 = (bf16[2,72,1728]{2,1,0:T(8,128)(2,1)S(1)}, bf16[2,72,1728]{2,1,0:T(8,128)(2,1)S(1)}, u32[]{:S(2)}, u32[]{:S(2)}) collective-permute-start(bf16[2,72,1728]{2,1,0:T(8,128)(2,1)S(1)} %get-tuple-element.54), channel_id=1, source_target_pairs={{0,2},{1,3},{2,0},{3,1},{4,6},{5,7},{6,4},{7,5},{8,10},{9,11},{10,... | collective-permute-start | bytes 1493000 | tf_op jit(solution)/shard_map/ppermute | solution.py:89
  538.8 42.7 %collective-permute-start.65 = (bf16[2,72,1728]{2,1,0:T(8,128)(2,1)S(1)}, bf16[2,72,1728]{2,1,0:T(8,128)(2,1)S(1)}, u32[]{:S(2)}, u32[]{:S(2)}) collective-permute-start(bf16[2,72,1728]{2,1,0:T(8,128)(2,1)S(1)} %get-tuple-element.60), channel_id=1, source_target_pairs={{0,2},{1,3},{2,0},{3,1},{4,6},{5,7},{6,4},{7,5},{8,10},{9,11},{10,... | collective-permute-start | bytes 1493000 | tf_op jit(solution)/shard_map/ppermute | solution.py:89
  548.4 44.2 %collective-permute-start.67 = (bf16[2,72,1728]{2,1,0:T(8,128)(2,1)S(1)}, bf16[2,72,1728]{2,1,0:T(8,128)(2,1)S(1)}, u32[]{:S(2)}, u32[]{:S(2)}) collective-permute-start(bf16[2,72,1728]{2,1,0:T(8,128)(2,1)S(1)} %get-tuple-element.63), channel_id=1, source_target_pairs={{0,2},{1,3},{2,0},{3,1},{4,6},{5,7},{6,4},{7,5},{8,10},{9,11},{10,... | collective-permute-start | bytes 1493000 | tf_op jit(solution)/shard_map/ppermute | solution.py:89
  559.4 42.5 %collective-permute-start.69 = (bf16[2,72,1728]{2,1,0:T(8,128)(2,1)S(1)}, bf16[2,72,1728]{2,1,0:T(8,128)(2,1)S(1)}, u32[]{:S(2)}, u32[]{:S(2)}) collective-permute-start(bf16[2,72,1728]{2,1,0:T(8,128)(2,1)S(1)} %get-tuple-element.62), channel_id=1, source_target_pairs={{0,2},{1,3},{2,0},{3,1},{4,6},{5,7},{6,4},{7,5},{8,10},{9,11},{10,... | collective-permute-start | bytes 1493000 | tf_op jit(solution)/shard_map/ppermute | solution.py:89
  581.6 25.3 %collective-permute-start.75 = (bf16[2,72,1728]{2,1,0:T(8,128)(2,1)S(1)}, bf16[2,72,1728]{2,1,0:T(8,128)(2,1)S(1)}, u32[]{:S(2)}, u32[]{:S(2)}) collective-permute-start(bf16[2,72,1728]{2,1,0:T(8,128)(2,1)S(1)} %get-tuple-element.50), channel_id=1, source_target_pairs={{0,4},{1,5},{2,6},{3,7},{4,8},{5,9},{6,10},{7,11},{8,12},{9,13},{1... | collective-permute-start | bytes 1493000 | tf_op jit(solution)/shard_map/ppermute | solution.py:89
  592.6 25.4 %collective-permute-start.77 = (bf16[2,72,1728]{2,1,0:T(8,128)(2,1)S(1)}, bf16[2,72,1728]{2,1,0:T(8,128)(2,1)S(1)}, u32[]{:S(2)}, u32[]{:S(2)}) collective-permute-start(bf16[2,72,1728]{2,1,0:T(8,128)(2,1)S(1)} %get-tuple-element.52), channel_id=1, source_target_pairs={{0,8},{1,9},{2,10},{3,11},{4,12},{5,13},{6,14},{7,15},{8,0},{9,1},... | collective-permute-start | bytes 1493000 | tf_op jit(solution)/shard_map/ppermute | solution.py:89
  602.0 33.5 %collective-permute-start.79 = (bf16[2,72,1728]{2,1,0:T(8,128)(2,1)S(1)}, bf16[2,72,1728]{2,1,0:T(8,128)(2,1)S(1)}, u32[]{:S(2)}, u32[]{:S(2)}) collective-permute-start(bf16[2,72,1728]{2,1,0:T(8,128)(2,1)S(1)} %get-tuple-element.51), channel_id=1, source_target_pairs={{0,12},{1,13},{2,14},{3,15},{4,0},{5,1},{6,2},{7,3},{8,4},{9,5},{1... | collective-permute-start | bytes 1493000 | tf_op jit(solution)/shard_map/ppermute | solution.py:89
  605.7 76.3 %collective-permute-start.71 = (bf16[2,72,1728]{2,1,0:T(8,128)(2,1)S(1)}, bf16[2,72,1728]{2,1,0:T(8,128)(2,1)S(1)}, u32[]{:S(2)}, u32[]{:S(2)}) collective-permute-start(bf16[2,72,1728]{2,1,0:T(8,128)(2,1)S(1)} %get-tuple-element.61), channel_id=1, source_target_pairs={{0,2},{1,3},{2,0},{3,1},{4,6},{5,7},{6,4},{7,5},{8,10},{9,11},{10,... | collective-permute-start | bytes 1493000 | tf_op jit(solution)/shard_map/ppermute | solution.py:89
  606.9 29.0 %collective-permute-start.84 = (bf16[216,1152]{1,0:T(8,128)(2,1)S(1)}, bf16[216,1152]{1,0:T(8,128)(2,1)S(1)}, u32[]{:S(2)}, u32[]{:S(2)}) collective-permute-start(bf16[216,1152]{1,0:T(8,128)(2,1)S(1)} %get-tuple-element.64), channel_id=1, source_target_pairs={{0,4},{1,5},{2,6},{3,7},{4,8},{5,9},{6,10},{7,11},{8,12},{9,13},{1... | collective-permute-start | bytes 1493000 | tf_op jit(solution)/shard_map/ppermute | solution.py:89
  618.0 41.6 %collective-permute-start.86 = (bf16[216,1152]{1,0:T(8,128)(2,1)S(1)}, bf16[216,1152]{1,0:T(8,128)(2,1)S(1)}, u32[]{:S(2)}, u32[]{:S(2)}) collective-permute-start(bf16[216,1152]{1,0:T(8,128)(2,1)S(1)} %get-tuple-element.66), channel_id=1, source_target_pairs={{0,8},{1,9},{2,10},{3,11},{4,12},{5,13},{6,14},{7,15},{8,0},{9,1},... | collective-permute-start | bytes 1493000 | tf_op jit(solution)/shard_map/ppermute | solution.py:89
  635.5 45.2 %collective-permute-start.88 = (bf16[216,1152]{1,0:T(8,128)(2,1)S(1)}, bf16[216,1152]{1,0:T(8,128)(2,1)S(1)}, u32[]{:S(2)}, u32[]{:S(2)}) collective-permute-start(bf16[216,1152]{1,0:T(8,128)(2,1)S(1)} %get-tuple-element.65), channel_id=1, source_target_pairs={{0,12},{1,13},{2,14},{3,15},{4,0},{5,1},{6,2},{7,3},{8,4},{9,5},{1... | collective-permute-start | bytes 1493000 | tf_op jit(solution)/shard_map/ppermute | solution.py:89
  635.9 82.6 %collective-permute-start.45 = (bf16[1024,1152]{1,0:T(8,128)(2,1)S(1)}, bf16[1024,1152]{1,0:T(8,128)(2,1)S(1)}, u32[]{:S(2)}, u32[]{:S(2)}) collective-permute-start(bf16[1024,1152]{1,0:T(8,128)(2,1)S(1)} %slice.269), channel_id=1, source_target_pairs={{0,1},{1,0},{2,3},{3,2},{4,5},{5,4},{6,7},{7,6},{8,9},{9,8},{10,11... | collective-permute-start | bytes 7077896 | tf_op jit(solution)/shard_map/ppermute | solution.py:92
  635.9 47.7 %collective-permute-start.66 = (bf16[2,72,1728]{2,1,0:T(8,128)(2,1)S(1)}, bf16[2,72,1728]{2,1,0:T(8,128)(2,1)S(1)}, u32[]{:S(2)}, u32[]{:S(2)}) collective-permute-start(bf16[2,72,1728]{2,1,0:T(8,128)(2,1)S(1)} %get-tuple-element.57), channel_id=1, source_target_pairs={{0,4},{1,5},{2,6},{3,7},{4,8},{5,9},{6,10},{7,11},{8,12},{9,13},{1... | collective-permute-start | bytes 1493000 | tf_op jit(solution)/shard_map/ppermute | solution.py:89
  659.6 43.5 %collective-permute-start.68 = (bf16[2,72,1728]{2,1,0:T(8,128)(2,1)S(1)}, bf16[2,72,1728]{2,1,0:T(8,128)(2,1)S(1)}, u32[]{:S(2)}, u32[]{:S(2)}) collective-permute-start(bf16[2,72,1728]{2,1,0:T(8,128)(2,1)S(1)} %get-tuple-element.59), channel_id=1, source_target_pairs={{0,8},{1,9},{2,10},{3,11},{4,12},{5,13},{6,14},{7,15},{8,0},{9,1},... | collective-permute-start | bytes 1493000 | tf_op jit(solution)/shard_map/ppermute | solution.py:89
  680.6 33.2 %collective-permute-start.70 = (bf16[2,72,1728]{2,1,0:T(8,128)(2,1)S(1)}, bf16[2,72,1728]{2,1,0:T(8,128)(2,1)S(1)}, u32[]{:S(2)}, u32[]{:S(2)}) collective-permute-start(bf16[2,72,1728]{2,1,0:T(8,128)(2,1)S(1)} %get-tuple-element.58), channel_id=1, source_target_pairs={{0,12},{1,13},{2,14},{3,15},{4,0},{5,1},{6,2},{7,3},{8,4},{9,5},{1... | collective-permute-start | bytes 1493000 | tf_op jit(solution)/shard_map/ppermute | solution.py:89
  682.0 36.3 %collective-permute-start.90 = (bf16[216,1152]{1,0:T(8,128)(2,1)S(1)}, bf16[216,1152]{1,0:T(8,128)(2,1)S(1)}, u32[]{:S(2)}, u32[]{:S(2)}) collective-permute-start(bf16[216,1152]{1,0:T(8,128)(2,1)S(1)} %fusion.58), channel_id=1, source_target_pairs={{0,16},{16,0},{1,17},{17,1},{2,18},{18,2},{3,19},{19,3},{4,20},{20... | collective-permute-start | bytes 1493000 | tf_op jit(solution)/shard_map/ppermute | solution.py:95
  683.6 30.7 %collective-permute-start.81 = (bf16[72,1728]{1,0:T(8,128)(2,1)S(1)}, bf16[72,1728]{1,0:T(8,128)(2,1)S(1)}, u32[]{:S(2)}, u32[]{:S(2)}) collective-permute-start(bf16[72,1728]{1,0:T(8,128)(2,1)S(1)} %dynamic-slice_bitcast_fusion.14), channel_id=1, source_target_pairs={{0,1},{1,0},{2,3},{3,2},{4,5},{5,4},{6,7},{7,6},{8,9},{9,8},{10,11... | collective-permute-start | bytes 746504 | tf_op jit(solution)/shard_map/ppermute | solution.py:92
  714.5 14.6 %collective-permute-start.82 = (bf16[2,72,1728]{2,1,0:T(8,128)(2,1)S(1)}, bf16[2,72,1728]{2,1,0:T(8,128)(2,1)S(1)}, u32[]{:S(2)}, u32[]{:S(2)}) collective-permute-start(bf16[2,72,1728]{2,1,0:T(8,128)(2,1)S(1)} %pad_maximum_fusion.17), channel_id=1, source_target_pairs={{0,16},{16,0},{1,17},{17,1},{2,18},{18,2},{3,19},{19,3},{4,20},{20... | collective-permute-start | bytes 1493000 | tf_op jit(solution)/shard_map/ppermute | solution.py:95
  716.9 23.2 %collective-permute-start.73 = (bf16[2,72,1728]{2,1,0:T(8,128)(2,1)}, bf16[2,72,1728]{2,1,0:T(8,128)(2,1)S(1)}, u32[]{:S(2)}, u32[]{:S(2)}) collective-permute-start(bf16[2,72,1728]{2,1,0:T(8,128)(2,1)} %pad_maximum_fusion.16), channel_id=1, source_target_pairs={{0,16},{16,0},{1,17},{17,1},{2,18},{18,2},{3,19},{19,3},{4,20},{20... | collective-permute-start | bytes 1493000 | tf_op jit(solution)/shard_map/ppermute | solution.py:95
  720.3 44.8 %collective-permute-start.46 = (bf16[512,1152]{1,0:T(8,128)(2,1)}, bf16[512,1152]{1,0:T(8,128)(2,1)}, u32[]{:S(2)}, u32[]{:S(2)}) collective-permute-start(bf16[512,1152]{1,0:T(8,128)(2,1)} %slice.271), channel_id=1, source_target_pairs={{0,16},{16,0},{1,17},{17,1},{2,18},{18,2},{3,19},{19,3},{4,20},{20... | collective-permute-start | bytes 3538952 | tf_op jit(solution)/shard_map/ppermute | solution.py:95
  815.0 41.5 %collective-permute-start.56 = (bf16[4,2,64,1152]{3,2,1,0:T(8,128)(2,1)}, bf16[4,2,64,1152]{3,2,1,0:T(8,128)(2,1)}, u32[]{:S(2)}, u32[]{:S(2)}) collective-permute-start(bf16[4,2,64,1152]{3,2,1,0:T(8,128)(2,1)} %dynamic-slice_bitcast_fusion.1), channel_id=1, source_target_pairs={{0,1},{1,0},{2,3},{3,2},{4,5},{5,4},{6,7},{7,6},{8,9},{9,8},{10,11... | collective-permute-start | bytes 3538952 | tf_op jit(solution)/shard_map/ppermute | solution.py:92
  834.4 28.0 %collective-permute-start.47 = (bf16[4,2,72,1664]{3,2,1,0:T(8,128)(2,1)}, bf16[4,2,72,1664]{3,2,1,0:T(8,128)(2,1)}, u32[]{:S(2)}, u32[]{:S(2)}) collective-permute-start(bf16[4,2,72,1664]{3,2,1,0:T(8,128)(2,1)} %dynamic-slice_bitcast_fusion), channel_id=1, source_target_pairs={{0,1},{1,0},{2,3},{3,2},{4,5},{5,4},{6,7},{7,6},{8,9},{9,8},{10,11... | collective-permute-start | bytes 5750792 | tf_op jit(solution)/shard_map/ppermute | solution.py:92
  861.2 28.5 %collective-permute-start.63 = (bf16[64,1152]{1,0:T(8,128)(2,1)S(1)}, bf16[64,1152]{1,0:T(8,128)(2,1)S(1)}, u32[]{:S(2)}, u32[]{:S(2)}) collective-permute-start(bf16[64,1152]{1,0:T(8,128)(2,1)S(1)} %get-tuple-element.92), channel_id=1, source_target_pairs={{0,2},{1,3},{2,0},{3,1},{4,6},{5,7},{6,4},{7,5},{8,10},{9,11},{10,... | collective-permute-start | bytes 442376 | tf_op jit(solution)/shard_map/ppermute | solution.py:89
  864.6 15.1 %collective-permute-start.48 = (bf16[72,1664]{1,0:T(8,128)(2,1)S(1)}, bf16[72,1664]{1,0:T(8,128)(2,1)S(1)}, u32[]{:S(2)}, u32[]{:S(2)}) collective-permute-start(bf16[72,1664]{1,0:T(8,128)(2,1)S(1)} %get-tuple-element.84), channel_id=1, source_target_pairs={{0,2},{1,3},{2,0},{3,1},{4,6},{5,7},{6,4},{7,5},{8,10},{9,11},{10,... | collective-permute-start | bytes 718856 | tf_op jit(solution)/shard_map/ppermute | solution.py:89
  865.4 19.4 %collective-permute-start.50 = (bf16[72,1664]{1,0:T(8,128)(2,1)S(1)}, bf16[72,1664]{1,0:T(8,128)(2,1)S(1)}, u32[]{:S(2)}, u32[]{:S(2)}) collective-permute-start(bf16[72,1664]{1,0:T(8,128)(2,1)S(1)} %get-tuple-element.87), channel_id=1, source_target_pairs={{0,2},{1,3},{2,0},{3,1},{4,6},{5,7},{6,4},{7,5},{8,10},{9,11},{10,... | collective-permute-start | bytes 718856 | tf_op jit(solution)/shard_map/ppermute | solution.py:89
  868.2 20.4 %collective-permute-start.52 = (bf16[72,1664]{1,0:T(8,128)(2,1)S(1)}, bf16[72,1664]{1,0:T(8,128)(2,1)S(1)}, u32[]{:S(2)}, u32[]{:S(2)}) collective-permute-start(bf16[72,1664]{1,0:T(8,128)(2,1)S(1)} %get-tuple-element.86), channel_id=1, source_target_pairs={{0,2},{1,3},{2,0},{3,1},{4,6},{5,7},{6,4},{7,5},{8,10},{9,11},{10,... | collective-permute-start | bytes 718856 | tf_op jit(solution)/shard_map/ppermute | solution.py:89
  871.5 18.8 %collective-permute-start.58 = (bf16[64,1152]{1,0:T(8,128)(2,1)S(1)}, bf16[64,1152]{1,0:T(8,128)(2,1)S(1)}, u32[]{:S(2)}, u32[]{:S(2)}) collective-permute-start(bf16[64,1152]{1,0:T(8,128)(2,1)S(1)} %get-tuple-element.88), channel_id=1, source_target_pairs={{0,4},{1,5},{2,6},{3,7},{4,8},{5,9},{6,10},{7,11},{8,12},{9,13},{1... | collective-permute-start | bytes 442376 | tf_op jit(solution)/shard_map/ppermute | solution.py:89
  890.4 17.9 %collective-permute-start.51 = (bf16[72,1664]{1,0:T(8,128)(2,1)S(1)}, bf16[72,1664]{1,0:T(8,128)(2,1)S(1)}, u32[]{:S(2)}, u32[]{:S(2)}) collective-permute-start(bf16[72,1664]{1,0:T(8,128)(2,1)S(1)} %get-tuple-element.83), channel_id=1, source_target_pairs={{0,8},{1,9},{2,10},{3,11},{4,12},{5,13},{6,14},{7,15},{8,0},{9,1},... | collective-permute-start | bytes 718856 | tf_op jit(solution)/shard_map/ppermute | solution.py:89
  891.9 16.4 %collective-permute-start.53 = (bf16[72,1664]{1,0:T(8,128)(2,1)S(1)}, bf16[72,1664]{1,0:T(8,128)(2,1)S(1)}, u32[]{:S(2)}, u32[]{:S(2)}) collective-permute-start(bf16[72,1664]{1,0:T(8,128)(2,1)S(1)} %get-tuple-element.82), channel_id=1, source_target_pairs={{0,12},{1,13},{2,14},{3,15},{4,0},{5,1},{6,2},{7,3},{8,4},{9,5},{1... | collective-permute-start | bytes 718856 | tf_op jit(solution)/shard_map/ppermute | solution.py:89
  893.8 16.3 %collective-permute-start.64 = (bf16[64,1152]{1,0:T(8,128)(2,1)S(1)}, bf16[64,1152]{1,0:T(8,128)(2,1)S(1)}, u32[]{:S(2)}, u32[]{:S(2)}) collective-permute-start(bf16[64,1152]{1,0:T(8,128)(2,1)S(1)} %fusion.70), channel_id=1, source_target_pairs={{0,16},{16,0},{1,17},{17,1},{2,18},{18,2},{3,19},{19,3},{4,20},{20... | collective-permute-start | bytes 442376 | tf_op jit(solution)/shard_map/ppermute | solution.py:95
  (150 other events, 1504.7 us)
